TPU v7x, 32 devices: a whole 2x2x4 slice. The times are simulated.
32 devices in a mesh: dp: 8 (over z, x), hyper: 4 (over y, core).
Axes of the slice: x: 2, y: 2, z: 4, core: 2. Of those that a mesh axis runs over, the one named last changes fastest.
Arguments:
- inputs: bfloat16 [64, 64, 128], P(('dp', 'hyper')), may hold values from -64 to 64
- labels: int32 [64, 64], P(('dp', 'hyper')), may hold values from 0 to 255
- client_ids: int32 [64], P(('dp', 'hyper')), may hold values from 0 to 63
- ext_weight: bfloat16 [128, 4096], replicated, may hold values from -0.5 to 0.5
- ext_bias: bfloat16 [4096], replicated, may hold values from -3 to 3
- embeddings: bfloat16 [64, 128], replicated, may hold values from -1.5 to 1.5
- hyper_in: bfloat16 [128, 50], replicated, may hold values from -2.09375 to 2.09375
- hyper_bias: float32 [50], replicated, may hold values from -3 to 3
- hyper_out: bfloat16 [4096, 50, 256], P('hyper'), may hold values from -0.1796875 to 0.1796875
Outputs:
- grad_ext_weight: float32 [128, 4096], replicated
- grad_ext_bias: float32 [4096], replicated
- grad_embeddings: float32 [64, 128], replicated
- grad_hyper_in: float32 [128, 50], replicated
- grad_hyper_bias: float32 [50], replicated
- grad_hyper_out: float32 [4096, 50, 256], P(('hyper', 'dp'))
Inputs may be any that keep to these rules, and one draw needn't show every extreme that they name: `client_ids`: A client may hold several slots or none.
All inputs are finite; a program needn't handle non-finite values.
Results may differ from a plain program's by a relative error of at most 0.014.
The roundings to bfloat16 on the way count: a program that leaves them out, or rounds other values in their place, can miss the bound.
Values may be sent and summed in bfloat16 or wider, within the bound.
A program may use at most 192 MiB of HBM per device.

v0:
```python
import jax
import jax.numpy as jnp
from jax import lax
from jax.sharding import PartitionSpec as P

highest = lax.Precision.HIGHEST
f32 = jnp.float32
bf16 = jnp.bfloat16


def silu_slope(values):
    logistic = jax.nn.sigmoid(values)
    return logistic * (1.0 + values * (1.0 - logistic))


def class_grads(logits, slot_labels, row_count):
    largest = jnp.max(logits, axis=-1, keepdims=True)
    exponent = jnp.exp(logits - largest)
    probability = exponent / jnp.sum(exponent, axis=-1, keepdims=True)
    classes = jnp.arange(logits.shape[-1], dtype=jnp.int32)
    onehot = (slot_labels[..., None] == classes).astype(f32)
    return ((probability - onehot) / row_count).astype(bf16)


def local(
    inputs, labels, client_ids, ext_weight, ext_bias, embeddings, hyper_in, hyper_bias, hyper_out
):
    everyone = ("dp", "hyper")
    n_dp, n_hyper = lax.axis_size("dp"), lax.axis_size("hyper")
    i, j = lax.axis_index("dp"), lax.axis_index("hyper")
    own, rows, width_in = inputs.shape
    wide = hyper_out.shape[0]
    narrow = wide // n_dp
    group = own * n_hyper
    slots = group * n_dp
    classes = hyper_out.shape[2]

    parts_of_ids = jnp.stack([client_ids // 256, client_ids % 256]).astype(bf16)
    flat_own = inputs.reshape(own * rows, width_in)
    packed = jnp.concatenate([flat_own, jnp.pad(parts_of_ids, ((0, 14), (0, width_in - own)))])
    from_group = lax.all_gather(packed, "hyper", axis=0)
    from_all = lax.all_gather(from_group, "dp", axis=0)
    table = jnp.arange(embeddings.shape[0], dtype=jnp.int32)

    def hypernet(gathered):
        gathered = gathered.reshape(-1, own * rows + 16, width_in)
        halves = gathered[:, own * rows : own * rows + 2, :own].astype(f32).astype(jnp.int32)
        ids = (halves[:, 0] * 256 + halves[:, 1]).reshape(-1)
        select = ids[:, None] == table[None, :]
        picked = jnp.dot(select.astype(bf16), embeddings, preferred_element_type=f32).astype(bf16)
        hyper_preact = jnp.dot(picked, hyper_in, preferred_element_type=f32) + hyper_bias
        hidden = jax.nn.silu(hyper_preact).astype(bf16)
        return select, picked, hyper_preact, hidden, gathered[:, : own * rows]

    hidden_group, in_group = hypernet(from_group)[3:]

    w_wide = lax.dynamic_slice_in_dim(ext_weight, j * wide, wide, 1)
    b_wide = lax.dynamic_slice_in_dim(ext_bias, j * wide, wide, 0).astype(f32)
    preact = jnp.dot(in_group.reshape(group * rows, width_in), w_wide, preferred_element_type=f32)
    features = jax.nn.silu(preact + b_wide).astype(bf16).reshape(group, rows, wide)
    heads = jnp.einsum("kh,dhc->kdc", hidden_group, hyper_out, preferred_element_type=f32)
    part = jnp.einsum("krd,kdc->krc", features, heads.astype(bf16), preferred_element_type=f32)
    parts = lax.all_to_all(
        part.reshape(n_hyper, own * rows, classes), "hyper", split_axis=0, concat_axis=0
    )
    logits = jnp.sum(parts, axis=0).reshape(own, rows, classes)
    dlogits = class_grads(logits, labels, rows)
    dlogits, from_all = lax.optimization_barrier((dlogits, from_all))
    select, picked, hyper_preact, hidden, in_all = hypernet(from_all)
    dl_all = lax.all_gather(dlogits, everyone, axis=0, tiled=True)

    start = (j * n_dp + i) * narrow
    w = lax.dynamic_slice_in_dim(ext_weight, start, narrow, 1)
    b = lax.dynamic_slice_in_dim(ext_bias, start, narrow, 0).astype(f32)
    out_rows = lax.dynamic_slice_in_dim(hyper_out, i * narrow, narrow, 0)
    out_rows = lax.optimization_barrier(out_rows)
    flat = in_all.reshape(slots * rows, width_in)
    preact = jnp.dot(flat, w, preferred_element_type=f32) + b
    features = jax.nn.silu(preact).astype(bf16).reshape(slots, rows, narrow)
    heads = jnp.einsum("kh,dhc->kdc", hidden, out_rows, preferred_element_type=f32).astype(bf16)
    dheads = jnp.einsum("krd,krc->kdc", features, dl_all, preferred_element_type=f32).astype(bf16)
    dfeatures = jnp.einsum("krc,kdc->krd", dl_all, heads, preferred_element_type=f32).astype(bf16)
    dpreact = (
        dfeatures.reshape(slots * rows, narrow).astype(f32) * silu_slope(preact)
    ).astype(bf16)
    grad_weight = jnp.dot(flat.T, dpreact, preferred_element_type=f32)
    grad_bias = jnp.sum(dpreact.astype(f32), axis=0)
    grad_out = jnp.einsum("kh,kdc->dhc", hidden, dheads, preferred_element_type=f32)
    dhidden = jnp.einsum("kdc,dhc->kh", dheads, out_rows, preferred_element_type=f32)
    bias_rows = jnp.zeros((n_hyper * n_dp, narrow), f32)
    bias_rows = lax.dynamic_update_slice_in_dim(bias_rows, grad_bias[None], j * n_dp + i, 0)
    dhidden, bias_rows = lax.psum((dhidden, bias_rows), everyone)
    hyper_dpre = dhidden * silu_slope(hyper_preact)
    grad_in = jnp.dot(picked.astype(f32).T, hyper_dpre, precision=highest)
    grad_hbias = jnp.sum(hyper_dpre, axis=0)
    back_rows = jnp.dot(hyper_dpre, hyper_in.astype(f32).T, precision=highest)
    grad_table = jnp.dot(select.astype(f32).T, back_rows, precision=highest)
    grad_weight = lax.all_gather(grad_weight, ("hyper", "dp"), axis=1, tiled=True)
    return (grad_weight, bias_rows.reshape(-1), grad_table, grad_in, grad_hbias, grad_out)


def solution(mesh):
    placed = (
        P(("dp", "hyper"), None, None),
        P(("dp", "hyper"), None),
        P(("dp", "hyper")),
        P(),
        P(),
        P(),
        P(),
        P(),
        P("hyper", None, None),
    )
    return jax.shard_map(
        local,
        mesh=mesh,
        in_specs=placed,
        out_specs=(P(), P(), P(), P(), P(), P(("hyper", "dp"), None, None)),
        check_vma=False,
    )
```

profile of v0, /device:TPU:0, one launch (start us, length us, event | category | flops | bytes accessed | tf_op | source)
XLA Modules:
  0.0 212.7 jit_solution(18060032566630711155)
XLA Ops:
  7.2 0.0 copy-start
  7.2 0.0 all-gather.10.cloned.1.call-start
  7.2 0.7 convert_bitcast_fusion
  8.0 0.8 pad_maximum_fusion
  8.8 7.1 %all-gather = bf16[576,128]{1,0:T(8,128)(2,1)} all-gather(bf16[144,128]{1,0:T(8,128)(2,1)S(1)} %pad_maximum_fusion), channel_id=2, replica_groups=mesh['dp'=8,'hyper'=4] {'hyper'}, dimensions={0}, use_global_device_ids=true | all-gather | bytes 184320 | tf_op jit(solution)/shard_map/all_gather | solution.py:41
  15.8 0.0 all-gather.10.cloned.1.call-update
  15.8 0.0 all-gather.6.cloned.1.call-start
  15.9 0.7 convert_convert_fusion.1
  16.6 0.1 add.113
  16.7 1.0 fusion.37
  17.7 29.1 %fusion.16 = bf16[8,1024,256]{2,0,1:T(8,128)(2,1)} fusion(bf16[8,50,1]{1,0,2:T(8,128)(2,1)S(1)} %fusion.37, bf16[1024,50,256]{2,0,1:T(8,128)(2,1)} %param.17), kind=kOutput, calls=%fused_computation.13 | convolution fusion | flops 211812352 | bytes 30409504 | tf_op jit(solution)/shard_map/kh,dhc->kdc/dot_general | solution.py:61
  46.8 0.7 dynamic-slice_convert_fusion
  47.5 0.7 multiply_convert_fusion.1
  48.3 1.5 copy-done.3
  49.7 0.9 fusion.6
  50.6 11.7 %all_to_all.5 = f32[4,128,256]{2,1,0:T(8,128)S(1)} all-to-all(f32[4,128,256]{2,1,0:T(8,128)S(1)} %bitcast.59), channel_id=1, replica_groups=mesh['dp'=8,'hyper'=4] {'hyper'}, dimensions={0} | all-to-all | bytes 1048576 | tf_op jit(solution)/shard_map/all_to_all | solution.py:63
  62.4 0.1 reduce_max.9
  62.5 0.1 sub.29
  62.5 0.2 exponential_reduce_fusion
  62.7 0.1 div.52
  62.8 0.8 multiply_convert_fusion.2
  63.6 0.0 all-gather.6.cloned.1.call-update
  63.6 0.0 all-gather.8.cloned.1.call-start
  63.7 4.1 %constant_dynamic-slice_fusion = bf16[128,50,256]{2,0,1:T(8,128)(2,1)} fusion(bf16[1024,50,256]{2,0,1:T(8,128)(2,1)} %param.17, s32[]{:T(128)S(6)} %select_n.29), kind=kLoop, calls=%fused_computation.69 | loop fusion | bytes 6553604 | tf_op jit(solution)/shard_map/dynamic_slice | solution.py:75
  67.8 0.8 dynamic-slice_convert_fusion.1
  68.6 0.1 slice.36
  68.7 0.1 fusion.26
  68.8 0.1 add.118
  68.9 0.2 convolution_convert_fusion.1
  69.1 0.1 convolution_add_fusion.1
  69.2 7.0 %fusion.13 = bf16[64,128,256]{2,0,1:T(8,128)(2,1)} fusion(bf16[128,50,256]{2,0,1:T(8,128)(2,1)} %constant_dynamic-slice_fusion, f32[64,50]{0,1:T(8,128)S(1)} %convolution_add_fusion.1), kind=kOutput, calls=%fused_computation.12 | convolution fusion | flops 211828352 | bytes 7483904 | tf_op jit(solution)/shard_map/kh,dhc->kdc/dot_general | solution.py:80
  76.2 44.1 %all-gather.6.cloned.1.call-done = bf16[64,64,256]{2,1,0:T(8,128)(2,1)} async-done(((bf16[2,64,256]{2,1,0:T(8,128)(2,1)}), bf16[64,64,256]{2,1,0:T(8,128)(2,1)}) %all-gather.6.cloned.1.call-update) | async-done | bytes 2097168 | tf_op jit(solution)/shard_map/all_gather | solution.py:70
  120.3 5.5 %fusion.20 = bf16[64,64,128]{2,1,0:T(8,128)(2,1)S(1)} fusion(bf16[64,64,256]{2,1,0:T(8,128)(2,1)} %all-gather.6.cloned.1.call-done, bf16[64,128,256]{2,0,1:T(8,128)(2,1)} %fusion.13), kind=kOutput, calls=%fused_computation.21 | convolution fusion | flops 268959744 | bytes 7340032 | tf_op jit(solution)/shard_map/krc,kdc->krd/dot_general | solution.py:82
  125.8 2.3 %convert_reduce_fusion = (f32[128]{0:T(128)S(1)}, bf16[4096,128]{1,0:T(8,128)(2,1)S(1)}, bf16[4096,128]{1,0:T(8,128)(2,1)}) fusion(bf16[64,64,128]{2,1,0:T(8,128)(2,1)S(1)} %fusion.20, f32[128]{0:T(128)S(1)} %dynamic-slice_convert_fusion.1, bf16[4096,128]{1,0:T(8,128)(2,1)S(1)} %bitcast.52, bf16[128,4096]{1,0:T(8,128)(2,1)S(1)} %copy-done, s32[]{:T(128)S(6)} %select_n.30), kind=kOutput, calls=%fused_computation.18 | convolution fusion | flops 142081920 | bytes 4228100 | tf_op jit(solution)/shard_map/dot_general | solution.py:78
  128.1 1.1 fusion.47
  129.3 0.0 all-gather.8.cloned.1.call-update
  129.3 6.4 %copy.28 = bf16[128,50,256]{0,1,2:T(8,128)(2,1)} copy(bf16[128,50,256]{2,0,1:T(8,128)(2,1)} %constant_dynamic-slice_fusion) | data formatting | bytes 6553600 | tf_op jit(solution)/shard_map/optimization_barrier | solution.py:76
  135.8 3.3 %convolution_convert_fusion = bf16[64,128,256]{2,1,0:T(8,128)(2,1)} fusion(bf16[64,64,128]{2,1,0:T(8,128)(2,1)S(1)} %bitcast.58, bf16[64,64,256]{2,1,0:T(8,128)(2,1)S(1)} %copy-done.2), kind=kOutput, calls=%fused_computation.14 | convolution fusion | flops 270532608 | bytes 7340032 | tf_op jit(solution)/shard_map/krd,krc->kdc/dot_general | solution.py:81
  139.1 6.6 %copy.27 = bf16[64,128,256]{1,0,2:T(8,128)(2,1)} copy(bf16[64,128,256]{2,1,0:T(8,128)(2,1)} %convolution_convert_fusion) | data formatting | bytes 8388608 | tf_op jit(solution)/shard_map/convert_element_type | solution.py:81
  145.7 5.4 %fusion.10 = f32[128,50,256]{2,1,0:T(8,128)S(1)} fusion(bf16[64,128,256]{2,1,0:T(8,128)(2,1)} %convolution_convert_fusion, f32[64,50]{0,1:T(8,128)S(1)} %convolution_add_fusion.1), kind=kOutput, calls=%fused_computation.11 | convolution fusion | flops 209731200 | bytes 10760704 | tf_op jit(solution)/shard_map/kh,kdc->dhc/dot_general | solution.py:88
  151.1 4.8 %copy.30 = f32[128,50,256]{2,0,1:T(8,128)} copy(f32[128,50,256]{2,1,0:T(8,128)S(1)} %fusion.10) | data formatting | bytes 13107200
  155.9 4.6 %convolution_bitcast_fusion = f32[64,50]{0,1:T(8,128)S(1)} fusion(bf16[64,128,256]{1,0,2:T(8,128)(2,1)} %copy.27, bf16[128,50,256]{0,1,2:T(8,128)(2,1)} %copy.28), kind=kOutput, calls=%fused_computation.22 | convolution fusion | flops 209715200 | bytes 7483904 | tf_op jit(solution)/shard_map/kdc,dhc->kh/dot_general | solution.py:89
  160.6 39.9 %all-reduce.1 = (f32[4096]{0:T(1024)}, f32[64,50]{0,1:T(8,128)S(1)}) all-reduce(f32[4096]{0:T(1024)S(1)} %bitcast.61, f32[64,50]{0,1:T(8,128)S(1)} %convolution_bitcast_fusion), channel_id=1, replica_groups=mesh['dp'=8,'hyper'=4] {'dp','hyper'}, use_global_device_ids=true, to_apply=%region_4.5 | all-reduce | flops 7296 | bytes 58368 | tf_op jit(solution)/shard_map/psum | solution.py:92
  200.5 0.6 fusion.45
  201.1 0.2 fusion.48
  201.4 0.9 fusion.25
  202.3 0.8 fusion.49
  203.0 3.1 %copy.51 = f32[128,4096]{1,0:T(8,128)} copy(f32[128,4096]{1,0:T(8,128)} %all-gather.8.cloned.1.call-done) | data formatting | bytes 4194304
  (29 shorter events, 0.2 us)
Async XLA Ops:
  7.2 40.4 %copy-start = (bf16[128,4096]{1,0:T(8,128)(2,1)S(1)}, bf16[128,4096]{1,0:T(8,128)(2,1)}, u32[]{:S(2)}) copy-start(bf16[128,4096]{1,0:T(8,128)(2,1)} %param.12) | copy-start | bytes 3145732
  7.2 56.4 %all-gather.10.cloned.1.call-start = ((), (), s32[]{:S(2)}) async-start(), calls=%async_computation.3 | async-start | bytes 1327104 | tf_op jit(solution)/shard_map/all_gather | solution.py:42
  15.8 104.5 %all-gather.6.cloned.1.call-start = ((), (), s32[]{:S(2)}) async-start(), calls=%async_computation.1 | async-start | bytes 2162688 | tf_op jit(solution)/shard_map/all_gather | solution.py:70
  17.7 29.1 %copy-start.4 = (bf16[576,128]{1,0:T(8,128)(2,1)S(1)}, bf16[576,128]{1,0:T(8,128)(2,1)}, u32[]{:S(2)}) copy-start(bf16[576,128]{1,0:T(8,128)(2,1)} %all-gather) | copy-start | bytes 442372
  47.5 2.2 %copy-start.3 = (bf16[8,1024,256]{2,0,1:T(8,128)(2,1)S(1)}, bf16[8,1024,256]{2,0,1:T(8,128)(2,1)}, u32[]{:S(2)}) copy-start(bf16[8,1024,256]{2,0,1:T(8,128)(2,1)} %fusion.16) | copy-start | bytes 12582916
  49.7 13.1 %copy-start.8 = (s32[2,64]{1,0:T(2,128)S(1)}, s32[2,64]{1,0:T(2,128)}, u32[]{:S(2)}) copy-start(s32[2,64]{1,0:T(2,128)} %param.10) | copy-start | bytes 1540
  63.6 139.4 %all-gather.8.cloned.1.call-start = ((), (), s32[]{:S(2)}) async-start(), calls=%async_computation.2 | async-start | bytes 2162688 | tf_op jit(solution)/shard_map/all_gather | solution.py:98
  63.7 4.9 %copy-start.6 = (bf16[32,144,128]{2,1,0:T(8,128)(2,1)S(1)}, bf16[32,144,128]{2,1,0:T(8,128)(2,1)}, u32[]{:S(2)}) copy-start(bf16[32,144,128]{2,1,0:T(8,128)(2,1)} %all-gather.10.cloned.1.call-done) | copy-start | bytes 3538948
  63.7 5.2 %copy-start.9 = (bf16[64,128]{1,0:T(8,128)(2,1)S(1)}, bf16[64,128]{1,0:T(8,128)(2,1)}, u32[]{:S(2)}) copy-start(bf16[64,128]{1,0:T(8,128)(2,1)} %param.14) | copy-start | bytes 49156
  63.7 5.4 %copy-start.7 = (bf16[128,50]{0,1:T(8,128)(2,1)S(1)}, bf16[128,50]{0,1:T(8,128)(2,1)}, u32[]{:S(2)}) copy-start(bf16[128,50]{0,1:T(8,128)(2,1)} %param.15) | copy-start | bytes 38404
  63.7 5.4 %copy-start.10 = (f32[50]{0:T(128)S(1)}, f32[50]{0:T(128)}, u32[]{:S(2)}) copy-start(f32[50]{0:T(128)} %param.16) | copy-start | bytes 604
  129.3 6.5 %copy-start.2 = (bf16[64,64,256]{2,1,0:T(8,128)(2,1)S(1)}, bf16[64,64,256]{2,1,0:T(8,128)(2,1)}, u32[]{:S(2)}) copy-start(bf16[64,64,256]{2,1,0:T(8,128)(2,1)} %all-gather.6.cloned.1.call-done) | copy-start | bytes 6291460
  129.3 6.5 %copy-start.5 = (bf16[4096,128]{1,0:T(8,128)(2,1)S(1)}, bf16[4096,128]{1,0:T(8,128)(2,1)}, u32[]{:S(2)}) copy-start(bf16[4096,128]{1,0:T(8,128)(2,1)} %get-tuple-element.34) | copy-start | bytes 3145732
  155.9 50.2 %copy-start.1 = (bf16[128,4096]{1,0:T(8,128)(2,1)S(1)}, bf16[128,4096]{1,0:T(8,128)(2,1)}, u32[]{:S(2)}) copy-start(bf16[128,4096]{1,0:T(8,128)(2,1)} %param.12) | copy-start | bytes 3145732
Sparse Core Ops, SparseCore 0:
  16.0 42.6 all-gather.9
  63.7 56.5 all-gather.5
  129.4 55.5 all-gather.7
where the time goes:
time: 213 us
  matrix products  63.2 us (30%)
  blocking collectives  58.7 us (28%)
  waiting for transfers between devices  44.1 us (21%)
  local copies, waits for them, and re-layouts  27.1 us (13%)
  between operations  13.9 us (7%)
  other arithmetic  5.5 us (3%)
    all_gather x1, waiting for transfers between devices, local(): dl_all = lax.all_gather(dlogits, everyone, axis=0, tiled=True)  44.1 us
    psum x1, blocking collectives, local(): dhidden, bias_rows = lax.psum((dhidden, bias_rows), everyone)  39.9 us
    dot_general x1, matrix products, local(): jnp.einsum('kh,dhc->kdc', hidden_group, hyper_out, preferred_element_type...  29.1 us
    all_to_all x1, blocking collectives, local(): lax.all_to_all(part.reshape(n_hyper, own * rows, classes), 'hyper', split...  11.7 us
    unnamed x24, local copies, waits for them, and re-layouts  9.45 us
    all_gather x1, blocking collectives, local(): from_group = lax.all_gather(packed, 'hyper', axis=0)  7.06 us
    dot_general x1, matrix products, local(): jnp.einsum('kh,dhc->kdc', hidden, out_rows, preferred_element_type=f32)  7.02 us
    convert_element_type x1, local copies, waits for them, and re-layouts, local(): jnp.einsum('krd,krc->kdc', features, dl_all, preferred_element_type=f32)  6.61 us
  transfers between devices with their start and end apart: 3, of which 1 were waited for; matrix products, arithmetic and copies ran while one was open for 38% of the time, Pallas kernels for 0%

commit v1 on v0

v1 whole, which is shorter than its diff:
```python
import functools

import jax
import jax.numpy as jnp
from jax import lax
from jax.experimental import pallas as pl
from jax.experimental.pallas import tpu as pltpu
from jax.sharding import PartitionSpec as P

highest = lax.Precision.HIGHEST
f32 = jnp.float32
bf16 = jnp.bfloat16
i32 = jnp.int32
VM = pl.BlockSpec(memory_space=pltpu.VMEM)
DG = 16
LIMIT = 60 * 1024 * 1024


def silu_slope(values):
    logistic = jax.nn.sigmoid(values)
    return logistic * (1.0 + values * (1.0 - logistic))


def dot(a, b, dims=((1,), (0,)), **kw):
    return lax.dot_general(a, b, (dims, ((), ())), preferred_element_type=f32, **kw)


def swap(index, other, count):
    if count & (count - 1):
        return lax.rem(index + other, count)
    out = index
    bit = 1
    while bit < count:
        if other & bit:
            out = out + bit - 2 * bit * lax.rem(index // bit, 2)
        bit *= 2
    return out


def source(index, other, count):
    if count & (count - 1):
        return lax.rem(index + count - other, count)
    return swap(index, other, count)


def place():
    i, j = lax.axis_index("dp"), lax.axis_index("hyper")
    return i, j, j + 1 - 2 * lax.rem(j, 2)


def barrier(i, j, n_dp, hyper_peers):
    sem = pltpu.get_barrier_semaphore()
    for t in range(1, n_dp):
        pl.semaphore_signal(sem, 1, device_id={"dp": swap(i, t, n_dp), "hyper": j})
    for peer in hyper_peers:
        pl.semaphore_signal(sem, 1, device_id={"dp": i, "hyper": peer})
    pl.semaphore_wait(sem, n_dp - 1 + len(hyper_peers))


def remote(src, dst, send, recv, dp, hyper):
    return pltpu.make_async_remote_copy(
        src_ref=src, dst_ref=dst, send_sem=send, recv_sem=recv, device_id={"dp": dp, "hyper": hyper}
    )


def gather_blocks(own, out, i, j, partner, n_dp, half, s1, r1, s2, r2, s3, r3):
    n_hyper = 2 * half
    sends = []

    def start(copy):
        copy.start()
        sends.append(copy)
        return copy

    first = {}
    for t in range(1, n_dp):
        first[t] = start(remote(own, out.at[i, j], s1.at[t], r1.at[t], swap(i, t, n_dp), j))
    second, third = {}, {}
    for t in range(n_dp):
        at = source(i, t, n_dp)
        if t:
            first[t].wait_recv()
        block = out.at[at, j] if t else own
        for u in range(1, half):
            second[t, u] = start(
                remote(block, out.at[at, j], s2.at[t, u], r2.at[t, u], i, lax.rem(j + 2 * u, n_hyper))
            )
        third[t, 0] = start(remote(block, out.at[at, j], s3.at[t, 0], r3.at[t, 0], i, partner))
    for t in range(n_dp):
        at = source(i, t, n_dp)
        for u in range(1, half):
            second[t, u].wait_recv()
            peer = lax.rem(j + n_hyper - 2 * u, n_hyper)
            third[t, u] = start(
                remote(out.at[at, peer], out.at[at, peer], s3.at[t, u], r3.at[t, u], i, partner)
            )
    for copy in third.values():
        copy.wait_recv()
    for copy in sends:
        copy.wait_send()


def gather_sems(n_dp, half):
    dma = pltpu.SemaphoreType.DMA
    return [dma((n_dp,)), dma((n_dp,))] + [dma((n_dp, half)) for _ in range(4)]


def same_parity(j, half):
    return [lax.rem(j + 2 * u, 2 * half) for u in range(1, half)]


def gather_kernel(n_dp, half, x_ref, out_ref, *sems):
    i, j, partner = place()
    barrier(i, j, n_dp, same_parity(j, half) + [partner])
    out_ref[i, j] = x_ref[...]
    gather_blocks(x_ref, out_ref, i, j, partner, n_dp, half, *sems)


def comm_params(number):
    return pltpu.CompilerParams(collective_id=number, has_side_effects=True, vmem_limit_bytes=LIMIT)


def gather_all(x, n_dp, n_hyper):
    return pl.pallas_call(
        functools.partial(gather_kernel, n_dp, n_hyper // 2),
        out_shape=jax.ShapeDtypeStruct((n_dp, n_hyper) + x.shape, x.dtype),
        in_specs=[VM],
        out_specs=VM,
        scratch_shapes=gather_sems(n_dp, n_hyper // 2),
        compiler_params=comm_params(0),
        name="gather_inputs",
    )(x)


def spread(hidden, kinds):
    k, h = hidden.shape
    rows = lax.broadcasted_iota(i32, (k * DG, k), 0) // DG
    pick = (rows == lax.broadcasted_iota(i32, (k * DG, k), 1)).astype(bf16)
    tall = dot(pick, hidden).astype(bf16)
    columns = lax.broadcasted_iota(i32, (h, h * DG), 1) // DG
    widen = (columns == lax.broadcasted_iota(i32, (h, h * DG), 0)).astype(bf16)
    full = dot(tall, widen)
    d = lax.broadcasted_iota(i32, full.shape, 0) % DG
    same = d == lax.broadcasted_iota(i32, full.shape, 1) % DG
    return jnp.where(same, full, 0.0).astype(bf16)


def spread_t(hidden):
    k, h = hidden.shape
    rows = lax.broadcasted_iota(i32, (h * DG, h), 0) // DG
    pick = (rows == lax.broadcasted_iota(i32, (h * DG, h), 1)).astype(bf16)
    tall = dot(pick, hidden, ((1,), (1,))).astype(bf16)
    columns = lax.broadcasted_iota(i32, (k, k * DG), 1) // DG
    widen = (columns == lax.broadcasted_iota(i32, (k, k * DG), 0)).astype(bf16)
    full = dot(tall, widen)
    d = lax.broadcasted_iota(i32, full.shape, 0) % DG
    same = d == lax.broadcasted_iota(i32, full.shape, 1) % DG
    return jnp.where(same, full, 0.0).astype(bf16)


def forward_kernel(own, rows, where_ref, x_ref, hid_ref, w_ref, b_ref, ho_ref, part_ref, diag, heads):
    step = pl.program_id(0)
    blocks = x_ref.shape[1]
    group = blocks * own
    wide = w_ref.shape[1]
    classes = ho_ref.shape[2]
    hh = ho_ref.shape[0]

    @pl.when(step == 0)
    def _():
        diag[...] = spread(hid_ref[...], None)
        part_ref[...] = jnp.zeros_like(part_ref)

    for g in range(wide // DG):
        rhs = ho_ref[:, g * DG : (g + 1) * DG, :].reshape(hh * DG, classes)
        out = dot(diag[...], rhs).astype(bf16)
        heads[:, g * DG : (g + 1) * DG, :] = out.reshape(group, DG, classes)
    for p in range(blocks):
        pre = dot(x_ref[0, p, : own * rows, :], w_ref[...]) + b_ref[...]
        feat = (pre / (1.0 + jnp.exp(-pre))).astype(bf16)
        for s in range(own):
            part_ref[p, s * rows : (s + 1) * rows, :] += dot(
                feat[s * rows : (s + 1) * rows], heads[p * own + s]
            )


def forward(where, gathered, hidden, ext_weight, ext_bias, ho, own, rows):
    n_dp, n_hyper, tall, width = gathered.shape
    hh, wide, classes = ho.shape
    chunk = 128
    group = own * n_hyper
    steps = wide // chunk
    return pl.pallas_call(
        functools.partial(forward_kernel, own, rows),
        out_shape=jax.ShapeDtypeStruct((n_hyper, own * rows, classes), f32),
        grid_spec=pltpu.PrefetchScalarGridSpec(
            num_scalar_prefetch=1,
            grid=(steps,),
            in_specs=[
                pl.BlockSpec((1, n_hyper, tall, width), lambda s, at: (at[0], 0, 0, 0)),
                pl.BlockSpec((group, hh), lambda s, at: (0, 0)),
                pl.BlockSpec((width, chunk), lambda s, at: (0, at[1] * steps + s)),
                pl.BlockSpec((1, chunk), lambda s, at: (0, at[1] * steps + s)),
                pl.BlockSpec((hh, chunk, classes), lambda s, at: (0, s, 0)),
            ],
            out_specs=pl.BlockSpec((n_hyper, own * rows, classes), lambda s, at: (0, 0, 0)),
            scratch_shapes=[
                pltpu.VMEM((group * DG, hh * DG), bf16),
                pltpu.VMEM((group, chunk, classes), bf16),
            ],
        ),
        compiler_params=pltpu.CompilerParams(vmem_limit_bytes=LIMIT),
        name="forward_part",
    )(where, gathered, hidden, ext_weight, ext_bias, ho)


def logits_kernel(n_dp, half, part, labels, out_ref, from_partner, summed, from_peer, own_dl, sp, rp, sq, rq, *sems):
    i, j, partner = place()
    n_hyper = 2 * half
    barrier(i, j, n_dp, same_parity(j, half) + [partner])
    to_partner = {}
    for u in list(range(1, half)) + [0]:
        to_partner[u] = remote(
            part.at[lax.rem(partner + 2 * u, n_hyper)], from_partner.at[u], sp.at[u], rp.at[u], i, partner
        )
        to_partner[u].start()
    to_peer = {}
    for u in range(1, half):
        peer = lax.rem(j + 2 * u, n_hyper)
        to_partner[u].wait_recv()
        summed[u] = part[peer] + from_partner[u]
        to_peer[u] = remote(summed.at[u], from_peer.at[u], sq.at[u], rq.at[u], i, peer)
        to_peer[u].start()
    to_partner[0].wait_recv()
    logits = part[j] + from_partner[0]
    for u in range(1, half):
        to_peer[u].wait_recv()
        logits = logits + from_peer[u]
    largest = jnp.max(logits, axis=-1, keepdims=True)
    exponent = jnp.exp(logits - largest)
    probability = exponent / jnp.sum(exponent, axis=-1, keepdims=True)
    onehot = (labels[...] == lax.broadcasted_iota(i32, logits.shape, 1)).astype(f32)
    dl = ((probability - onehot) / ROWS[0]).astype(bf16)
    own_dl[...] = dl
    out_ref[i, j] = dl
    gather_blocks(own_dl, out_ref, i, j, partner, n_dp, half, *sems)
    for copy in list(to_partner.values()) + list(to_peer.values()):
        copy.wait_send()


ROWS = [64]


def logits_and_gather(part, labels, n_dp, n_hyper, rows):
    half = n_hyper // 2
    _, tall, classes = part.shape
    dma = pltpu.SemaphoreType.DMA
    ROWS[0] = rows
    return pl.pallas_call(
        functools.partial(logits_kernel, n_dp, half),
        out_shape=jax.ShapeDtypeStruct((n_dp, n_hyper, tall, classes), bf16),
        in_specs=[VM, VM],
        out_specs=VM,
        scratch_shapes=[
            pltpu.VMEM((half, tall, classes), f32),
            pltpu.VMEM((half, tall, classes), f32),
            pltpu.VMEM((half, tall, classes), f32),
            pltpu.VMEM((tall, classes), bf16),
        ]
        + [dma((half,)) for _ in range(4)]
        + gather_sems(n_dp, half),
        compiler_params=comm_params(1),
        name="logits_exchange",
    )(part, labels)


def backward_kernel(own, rows, where_ref, dl_ref, x_ref, hid_ref, w_ref, b_ref, ho_ref,
                    gw_ref, gb_ref, go_ref, dh_ref, diag, diag_t, heads, dheads, feats, slopes, dpre, total):
    step = pl.program_id(0)
    dpc, n_hyper = dl_ref.shape[:2]
    hh, narrow, classes = ho_ref.shape
    width = x_ref.shape[3]
    groups = narrow // DG
    slots = dpc * n_hyper * own
    tall = own * rows
    hidden = hid_ref[...]
    diag[...] = spread(hidden, None)
    diag_t[...] = spread_t(hidden)

    @pl.when(step == 0)
    def _():
        gw_ref[...] = jnp.zeros_like(gw_ref)
        gb_ref[...] = jnp.zeros_like(gb_ref)
        go_ref[...] = jnp.zeros_like(go_ref)

    def ho_group(g):
        return ho_ref[:, pl.ds(pl.multiple_of(g * DG, DG), DG), :].reshape(hh * DG, classes)

    def heads_step(g, carry):
        out = dot(diag[...], ho_group(g)).astype(bf16)
        heads[:, pl.ds(pl.multiple_of(g * DG, DG), DG), :] = out.reshape(slots, DG, classes)
        return carry

    lax.fori_loop(0, groups, heads_step, 0)

    def features_step(a, carry):
        for p in range(n_hyper):
            pre = dot(x_ref[a, p, :tall, :], w_ref[...]) + b_ref[...]
            logistic = 1.0 / (1.0 + jnp.exp(-pre))
            at = pl.ds(pl.multiple_of((a * n_hyper + p) * tall, tall), tall)
            feats[at, :] = (pre * logistic).astype(bf16)
            slopes[at, :] = logistic * (1.0 + pre * (1.0 - logistic))
        return carry

    lax.fori_loop(0, dpc, features_step, 0)

    def slots_step(a, carry):
        for p in range(n_hyper):
            for s in range(own):
                block = a * n_hyper + p
                slot = block * own + s
                dl = dl_ref[a, p, s * rows : (s + 1) * rows, :]
                at = pl.ds(pl.multiple_of(block * tall + s * rows, rows), rows)
                dhead = dot(feats[at, :], dl, ((0,), (0,))).astype(bf16)
                dheads[:, pl.ds(pl.multiple_of(slot * DG, DG), DG), :] = dhead.reshape(groups, DG, classes)
                dfeat = dot(dl, heads[slot], ((1,), (1,))).astype(bf16)
                dpre[at, :] = (dfeat.astype(f32) * slopes[at, :]).astype(bf16)
        return carry

    lax.fori_loop(0, dpc, slots_step, 0)

    def weight_step(a, carry):
        gw, gb = carry
        for p in range(n_hyper):
            at = pl.ds(pl.multiple_of((a * n_hyper + p) * tall, tall), tall)
            block = dpre[at, :]
            gw = gw + dot(x_ref[a, p, :tall, :], block, ((0,), (0,)))
            gb = gb + jnp.sum(block.astype(f32), axis=0, keepdims=True)
        return gw, gb

    zero = (jnp.zeros((width, narrow), f32), jnp.zeros((1, narrow), f32))
    gw, gb = lax.fori_loop(0, dpc, weight_step, zero)
    gw_ref[...] += gw
    gb_ref[...] += gb
    total[...] = jnp.zeros_like(total)

    def out_step(g, carry):
        block = dheads[g]
        at = pl.ds(pl.multiple_of(g * DG, DG), DG)
        go_ref[:, at, :] += dot(diag_t[...], block).reshape(hh, DG, classes)
        total[...] += dot(block, ho_group(g), ((1,), (1,)))
        return carry

    lax.fori_loop(0, groups, out_step, 0)
    d = lax.broadcasted_iota(i32, total.shape, 0) % DG
    same = d == lax.broadcasted_iota(i32, total.shape, 1) % DG
    kept = jnp.where(same, total[...], 0.0).reshape(slots, DG, hh * DG)
    kept = jnp.sum(kept, axis=1)
    columns = lax.broadcasted_iota(i32, (hh * DG, hh), 0) // DG
    fold = (columns == lax.broadcasted_iota(i32, (hh * DG, hh), 1)).astype(f32)
    dh_ref[...] = dot(kept, fold, precision=highest)


def backward(where, dl_all, gathered, hidden, w, b, ho, own, rows):
    n_dp, n_hyper, tall, width = gathered.shape
    hh, wide, classes = ho.shape
    narrow = wide // n_dp
    group = own * n_hyper
    dpc = max(1, 64 // group)
    slots = dpc * group
    samples = slots * rows
    return pl.pallas_call(
        functools.partial(backward_kernel, own, rows),
        out_shape=(
            jax.ShapeDtypeStruct((width, narrow), f32),
            jax.ShapeDtypeStruct((1, narrow), f32),
            jax.ShapeDtypeStruct((hh, narrow, classes), f32),
            jax.ShapeDtypeStruct((n_dp * group, hh), f32),
        ),
        grid_spec=pltpu.PrefetchScalarGridSpec(
            num_scalar_prefetch=1,
            grid=(n_dp // dpc,),
            in_specs=[
                pl.BlockSpec((dpc, n_hyper, own * rows, classes), lambda s, at: (s, 0, 0, 0)),
                pl.BlockSpec((dpc, n_hyper, tall, width), lambda s, at: (s, 0, 0, 0)),
                pl.BlockSpec((slots, hh), lambda s, at: (s, 0)),
                pl.BlockSpec((width, narrow), lambda s, at: (0, 0)),
                pl.BlockSpec((1, narrow), lambda s, at: (0, 0)),
                pl.BlockSpec((hh, narrow, classes), lambda s, at: (0, at[0], 0)),
            ],
            out_specs=[
                pl.BlockSpec((width, narrow), lambda s, at: (0, 0)),
                pl.BlockSpec((1, narrow), lambda s, at: (0, 0)),
                pl.BlockSpec((hh, narrow, classes), lambda s, at: (0, 0, 0)),
                pl.BlockSpec((slots, hh), lambda s, at: (s, 0)),
            ],
            scratch_shapes=[
                pltpu.VMEM((slots * DG, hh * DG), bf16),
                pltpu.VMEM((hh * DG, slots * DG), bf16),
                pltpu.VMEM((slots, narrow, classes), bf16),
                pltpu.VMEM((narrow // DG, slots * DG, classes), bf16),
                pltpu.VMEM((samples, narrow), bf16),
                pltpu.VMEM((samples, narrow), f32),
                pltpu.VMEM((samples, narrow), bf16),
                pltpu.VMEM((slots * DG, hh * DG), f32),
            ],
        ),
        compiler_params=pltpu.CompilerParams(vmem_limit_bytes=LIMIT),
        name="backward_part",
    )(where, dl_all, gathered, hidden, w, b, ho)


def final_kernel(n_dp, half, x_ref, dh_ref, out_ref, tot_ref, b1, b2, mine, sa, ra, sb, rb, sc, rc, *sems):
    i, j, partner = place()
    n_hyper = 2 * half
    peers = [lax.rem(j + u, n_hyper) for u in range(1, n_hyper)]
    barrier(i, j, n_dp, peers)
    sends = []
    to_hyper = []
    for u in range(1, n_hyper):
        copy = remote(dh_ref.at[peers[u - 1]], b1.at[u], sa.at[u], ra.at[u], i, peers[u - 1])
        copy.start()
        to_hyper.append(copy)
    out_ref[i, j] = x_ref[...]
    quarter = dh_ref[j]
    for u in range(1, n_hyper):
        to_hyper[u - 1].wait_recv()
        quarter = quarter + b1[u]
    mine[0] = quarter
    b2[i] = quarter
    to_dp = []
    for t in range(1, n_dp):
        copy = remote(mine.at[0], b2.at[i], sb.at[t], rb.at[t], swap(i, t, n_dp), j)
        copy.start()
        to_dp.append(copy)
    gather_blocks(x_ref, out_ref, i, j, partner, n_dp, half, *sems)
    for copy in to_dp:
        copy.wait_recv()
    total = b2[0]
    for t in range(1, n_dp):
        total = total + b2[t]
    mine[1] = total
    tot_ref[j] = total
    last = []
    for u in range(1, n_hyper):
        copy = remote(mine.at[1], tot_ref.at[j], sc.at[u], rc.at[u], i, peers[u - 1])
        copy.start()
        last.append(copy)
    for copy in last:
        copy.wait_recv()
    for copy in to_hyper + to_dp + last:
        copy.wait_send()


def final_exchange(x, dh, n_dp, n_hyper):
    dma = pltpu.SemaphoreType.DMA
    part = dh.shape[1:]
    return pl.pallas_call(
        functools.partial(final_kernel, n_dp, n_hyper // 2),
        out_shape=(
            jax.ShapeDtypeStruct((n_dp, n_hyper) + x.shape, x.dtype),
            jax.ShapeDtypeStruct(dh.shape, f32),
        ),
        in_specs=[VM, VM],
        out_specs=(VM, VM),
        scratch_shapes=[
            pltpu.VMEM((n_hyper,) + part, f32),
            pltpu.VMEM((n_dp,) + part, f32),
            pltpu.VMEM((2,) + part, f32),
            dma((n_hyper,)), dma((n_hyper,)), dma((n_dp,)), dma((n_dp,)), dma((n_hyper,)), dma((n_hyper,)),
        ]
        + gather_sems(n_dp, n_hyper // 2),
        compiler_params=comm_params(2),
        name="final_exchange",
    )(x, dh)


def local(
    inputs, labels, client_ids, ext_weight, ext_bias, embeddings, hyper_in, hyper_bias, hyper_out
):
    n_dp, n_hyper = lax.axis_size("dp"), lax.axis_size("hyper")
    i, j = lax.axis_index("dp"), lax.axis_index("hyper")
    own, rows, width_in = inputs.shape
    wide, hh, classes = hyper_out.shape
    narrow = wide // n_dp
    group = own * n_hyper
    slots = group * n_dp
    tall = own * rows

    parts_of_ids = jnp.stack([client_ids // 256, client_ids % 256]).astype(bf16)
    flat_own = inputs.reshape(tall, width_in)
    packed = jnp.concatenate([flat_own, jnp.pad(parts_of_ids, ((0, 14), (0, width_in - own)))])
    gathered = gather_all(packed, n_dp, n_hyper)
    table = jnp.arange(embeddings.shape[0], dtype=i32)
    halves = gathered[:, :, tall : tall + 2, :own].astype(f32).astype(i32)
    ids = (halves[:, :, 0] * 256 + halves[:, :, 1]).reshape(-1)
    select = ids[:, None] == table[None, :]
    picked = jnp.dot(select.astype(bf16), embeddings, preferred_element_type=f32).astype(bf16)
    hyper_preact = jnp.dot(picked, hyper_in, preferred_element_type=f32) + hyper_bias
    hidden = jax.nn.silu(hyper_preact).astype(bf16)

    where = jnp.stack([i, j]).astype(i32)
    ho = hyper_out.transpose(1, 0, 2)
    wide_bias = ext_bias.astype(f32)[None]
    hidden_group = lax.dynamic_slice_in_dim(hidden, i * group, group, 0)
    part = forward(where, gathered, hidden_group, ext_weight, wide_bias, ho, own, rows)
    dl_all = logits_and_gather(part, labels.reshape(tall, 1), n_dp, n_hyper, rows)

    start = (j * n_dp + i) * narrow
    w = lax.dynamic_slice_in_dim(ext_weight, start, narrow, 1)
    b = lax.dynamic_slice_in_dim(wide_bias, start, narrow, 1)
    gw, gb, grad_out, dh = backward(where, dl_all, gathered, hidden, w, b, ho, own, rows)
    sent = jnp.concatenate([gw, jnp.pad(gb, ((0, 15), (0, 0)))]).astype(bf16)
    dh = jnp.pad(dh, ((0, 0), (0, 128 - hh))).reshape(n_hyper, slots // n_hyper, 128)
    gw_all, dhidden = final_exchange(sent, dh, n_dp, n_hyper)
    dhidden = dhidden.reshape(slots, 128)[:, :hh]
    hyper_dpre = dhidden * silu_slope(hyper_preact)
    grad_in = jnp.dot(picked.astype(f32).T, hyper_dpre, precision=highest)
    grad_hbias = jnp.sum(hyper_dpre, axis=0)
    back_rows = jnp.dot(hyper_dpre, hyper_in.astype(f32).T, precision=highest)
    grad_table = jnp.dot(select.astype(f32).T, back_rows, precision=highest)
    grad_weight = gw_all[:, :, :width_in].transpose(2, 1, 0, 3).reshape(width_in, -1).astype(f32)
    grad_bias = gw_all[:, :, width_in].transpose(1, 0, 2).reshape(-1).astype(f32)
    return (grad_weight, grad_bias, grad_table, grad_in, grad_hbias, grad_out.transpose(1, 0, 2))


def solution(mesh):
    placed = (
        P(("dp", "hyper"), None, None),
        P(("dp", "hyper"), None),
        P(("dp", "hyper")),
        P(),
        P(),
        P(),
        P(),
        P(),
        P("hyper", None, None),
    )
    return jax.shard_map(
        local,
        mesh=mesh,
        in_specs=placed,
        out_specs=(P(), P(), P(), P(), P(), P(("hyper", "dp"), None, None)),
        check_vma=False,
    )
```

time: 213 us -> 146 us (0.69)
  Pallas kernels: 0 us -> 120 us
  matrix products: 63.2 us -> 2.92 us
  blocking collectives: 58.7 us -> 0 us
  waiting for transfers between devices: 44.1 us -> 0 us
  local copies, waits for them, and re-layouts: 27.1 us -> 10.8 us
  between operations: 13.9 us -> 0.74 us
  other arithmetic: 5.5 us -> 10 us
    pallas_call x0 -> x5, Pallas kernels: none -> 120 us  [the longest x1 31 us: backward(): pl.pallas_call(functools.partial(backward_kernel, own, rows), out_shape=(...]
    dot_general x13 -> x2, matrix products: 61.3 us -> 1.05 us  [the longest x1 0.86 us: local(): jnp.dot(picked, hyper_in, preferred_element_type=f32) + hyper_bias]
    all_gather x3 -> x0, waiting for transfers between devices: 44.1 us -> none  [the longest x1 44.1 us: local(): dl_all = lax.all_gather(dlogits, everyone, axis=0, tiled=True)]
    psum x1 -> x0, blocking collectives: 39.9 us -> none  [local(): dhidden, bias_rows = lax.psum((dhidden, bias_rows), everyone)]
    all_to_all x1 -> x0, blocking collectives: 11.7 us -> none  [local(): lax.all_to_all(part.reshape(n_hyper, own * rows, classes), 'hyper', split...]
    all_gather x1 -> x0, blocking collectives: 7.06 us -> none  [local(): from_group = lax.all_gather(packed, 'hyper', axis=0)]
    unnamed x24 -> x9, local copies, waits for them, and re-layouts: 9.45 us -> 2.9 us
    optimization_barrier x1 -> x0, local copies, waits for them, and re-layouts: 6.44 us -> none  [local(): out_rows = lax.optimization_barrier(out_rows)]
  transfers between devices with their start and end apart: 3 -> 0, of which waited for: 1 -> 0; matrix products, arithmetic and copies ran while one was open for 38% -> 0% of each run, Pallas kernels for 0% -> 0%
where the time goes in v1:
time: 146 us; the launch traced here: 145 us
  Pallas kernels  120 us (82%)
  local copies, waits for them, and re-layouts  10.8 us (7%)
  other arithmetic  10 us (7%)
  matrix products  2.92 us (2%)
    pallas_call x1, Pallas kernels, backward(): pl.pallas_call(functools.partial(backward_kernel, own, rows), out_shape=(...  31 us
    pallas_call x1, Pallas kernels, logits_and_gather(): pl.pallas_call(functools.partial(logits_kernel, n_dp, half), out_shape=ja...  28.5 us
    pallas_call x1, Pallas kernels, final_exchange(): pl.pallas_call(functools.partial(final_kernel, n_dp, n_hyper // 2), out_s...  24 us
    pallas_call x1, Pallas kernels, gather_all(): pl.pallas_call(functools.partial(gather_kernel, n_dp, n_hyper // 2), out_...  20.1 us
    pallas_call x1, Pallas kernels, forward(): pl.pallas_call(functools.partial(forward_kernel, own, rows), out_shape=ja...  16.9 us

profile of v1, /device:TPU:0, one launch (start us, length us, event | category | flops | bytes accessed | tf_op | source)
XLA Modules:
  0.0 145.0 jit_solution(9057104523099459676)
XLA Ops:
  0.6 0.0 copy-start
  0.7 0.6 pad_add_fusion.where_ref
  1.3 0.7 convert_bitcast_fusion.1
  1.9 0.7 convert_element_type.52
  2.6 0.0 copy-start.1
  2.6 0.6 dynamic-slice_bitcast_fusion.b_ref
  3.2 1.4 constant_dynamic-slice_fusion.w_ref
  4.6 1.4 pad_maximum_fusion.x_ref
  6.0 1.4 reshape.54.labels
  7.4 20.1 %gather_inputs.1.x_ref = bf16[8,4,144,128]{3,2,1,0:T(8,128)(2,1)} custom-call(bf16[144,128]{1,0:T(8,128)(2,1)} %pad_maximum_fusion.x_ref), custom_call_target="tpu_custom_call" | custom-call | tf_op jit(solution)/shard_map/gather_inputs/pallas_call | solution.py:124
  27.6 0.9 convert_convert_fusion
  28.4 0.1 fusion.3
  28.5 0.1 add.51
  28.6 0.0 copy-done
  28.6 0.2 convolution_convert_fusion
  28.8 0.9 multiply_convert_fusion
  29.7 0.0 copy-start.2
  29.7 0.6 constant_dynamic-slice_fusion.1.hid_ref
  30.3 0.0 copy-done.1
  30.3 16.9 %forward_part.1.part = f32[4,128,256]{2,1,0:T(8,128)} custom-call(s32[2]{0:T(128)} %pad_add_fusion.where_ref, bf16[8,4,144,128]{3,2,1,0:T(8,128)(2,1)} %gather_inputs.1.x_ref, bf16[8,50]{1,0:T(8,128)(2,1)} %constant_dynamic-slice_fusion.1.hid_ref, bf16[128,4096]{1,0:T(8,128)(2,1)} %w_ref.1, f32[1,4096]{1,0:T(1,128)} %bitcast.35, bf16[50,1024,256]{2,1,0:T(8,128)(2,1)} %bitcast.31), custom_call_target="tpu_custom_call" | custom-call | tf_op jit(solution)/shard_map/forward_part/pallas_call | solution.py:193
  47.2 0.0 copy-done.2
  47.2 28.5 %logits_exchange.1.dl_ref = bf16[8,4,128,256]{3,2,1,0:T(8,128)(2,1)} custom-call(f32[4,128,256]{2,1,0:T(8,128)} %forward_part.1.part, s32[128,1]{1,0:T(8,128)} %reshape.54.labels), custom_call_target="tpu_custom_call" | custom-call | tf_op jit(solution)/shard_map/logits_exchange/pallas_call | solution.py:259
  75.7 0.0 copy-start.3
  75.7 31.0 %backward_part.1 = (f32[128,128]{1,0:T(8,128)}, f32[1,128]{1,0:T(1,128)}, f32[50,128,256]{2,1,0:T(8,128)}, f32[64,50]{1,0:T(8,128)}) custom-call(s32[2]{0:T(128)} %pad_add_fusion.where_ref, bf16[8,4,128,256]{3,2,1,0:T(8,128)(2,1)} %logits_exchange.1.dl_ref, bf16[8,4,144,128]{3,2,1,0:T(8,128)(2,1)} %gather_inputs.1.x_ref, bf16[64,50]{1,0:T(8,128)(2,1)} %copy-done.2, ...), custom_call_target="tpu_custom_call" | custom-call | tf_op jit(solution)/shard_map/backward_part/pallas_call | solution.py:372
  106.7 0.8 convert.23
  107.5 0.7 convert.24
  108.2 0.6 fusion.1.x_ref
  108.8 1.4 pad.15
  110.2 24.0 %final_exchange.1 = (bf16[8,4,144,128]{3,2,1,0:T(8,128)(2,1)}, f32[4,16,128]{2,1,0:T(8,128)}) custom-call(bf16[144,128]{1,0:T(8,128)(2,1)} %fusion.1.x_ref, f32[4,16,128]{2,1,0:T(8,128)} %bitcast.34), custom_call_target="tpu_custom_call" | custom-call | tf_op jit(solution)/shard_map/final_exchange/pallas_call | solution.py:458
  134.2 1.3 fusion.14
  135.5 0.8 fusion.16
  136.3 0.0 copy-done.3
  136.3 0.1 fusion.15
  136.5 0.9 fusion.2
  137.4 0.8 slice_convert_fusion
  138.2 0.6 copy.24
  138.8 1.5 %convert_bitcast_fusion = f32[128,4,8,128]{3,0,1,2:T(8,128)S(1)} fusion(bf16[8,4,144,128]{3,2,1,0:T(8,128)(2,1)} %get-tuple-element.15), kind=kLoop, calls=%fused_computation | loop fusion | flops 524288 | bytes 3145728 | tf_op jit(solution)/shard_map/convert_element_type | solution.py:522
  140.3 1.9 %copy.19 = f32[128,4,8,128]{0,3,2,1:T(8,128)} copy(f32[128,4,8,128]{3,0,1,2:T(8,128)S(1)} %convert_bitcast_fusion) | data formatting | bytes 4194304 | tf_op jit(solution)/shard_map/convert_element_type | solution.py:522
  142.1 2.9 %copy.21 = f32[128,4096]{1,0:T(8,128)} copy(f32[128,4096]{0,1:T(8,128)} %bitcast.33) | data formatting | bytes 4194304
  (1 shorter events, 0.0 us)
Async XLA Ops:
  0.6 28.0 %copy-start = (bf16[64,128]{1,0:T(8,128)(2,1)S(1)}, bf16[64,128]{1,0:T(8,128)(2,1)}, u32[]{:S(2)}) copy-start(bf16[64,128]{1,0:T(8,128)(2,1)} %param.14) | copy-start | bytes 49156
  2.6 27.6 %copy-start.1 = (f32[4096]{0:T(1024)}, f32[4096]{0:T(1024)S(1)}, u32[]{:S(2)}) copy-start(f32[4096]{0:T(1024)S(1)} %convert_element_type.52) | copy-start | bytes 49156
  29.7 17.5 %copy-start.2 = (bf16[64,50]{1,0:T(8,128)(2,1)}, bf16[64,50]{1,0:T(8,128)(2,1)S(1)}, u32[]{:S(2)}) copy-start(bf16[64,50]{1,0:T(8,128)(2,1)S(1)} %get-tuple-element.28.hid_ref) | copy-start | bytes 19204
  75.7 60.6 %copy-start.3 = (bf16[128,50]{0,1:T(8,128)(2,1)S(1)}, bf16[128,50]{0,1:T(8,128)(2,1)}, u32[]{:S(2)}) copy-start(bf16[128,50]{0,1:T(8,128)(2,1)} %param.15) | copy-start | bytes 38404

commit v2 on v0

v2 whole, which is shorter than its diff:
```python
import functools

import jax
import jax.numpy as jnp
from jax import lax
from jax.experimental import pallas as pl
from jax.experimental.pallas import tpu as pltpu
from jax.sharding import PartitionSpec as P

highest = lax.Precision.HIGHEST
f32 = jnp.float32
bf16 = jnp.bfloat16
i32 = jnp.int32
VM = pl.BlockSpec(memory_space=pltpu.VMEM)
DG = 16
LIMIT = 60 * 1024 * 1024


def silu_slope(values):
    logistic = jax.nn.sigmoid(values)
    return logistic * (1.0 + values * (1.0 - logistic))


def dot(a, b, dims=((1,), (0,)), **kw):
    return lax.dot_general(a, b, (dims, ((), ())), preferred_element_type=f32, **kw)


def swap(index, other, count):
    if count & (count - 1):
        return lax.rem(index + other, count)
    out = index
    bit = 1
    while bit < count:
        if other & bit:
            out = out + bit - 2 * bit * lax.rem(index // bit, 2)
        bit *= 2
    return out


def source(index, other, count):
    if count & (count - 1):
        return lax.rem(index + count - other, count)
    return swap(index, other, count)


def place():
    i, j = lax.axis_index("dp"), lax.axis_index("hyper")
    return i, j, j + 1 - 2 * lax.rem(j, 2)


def spread(hidden):
    k, h = hidden.shape
    rows = lax.broadcasted_iota(i32, (k * DG, k), 0) // DG
    pick = (rows == lax.broadcasted_iota(i32, (k * DG, k), 1)).astype(bf16)
    tall = dot(pick, hidden).astype(bf16)
    columns = lax.broadcasted_iota(i32, (h, h * DG), 1) // DG
    widen = (columns == lax.broadcasted_iota(i32, (h, h * DG), 0)).astype(bf16)
    full = dot(tall, widen)
    d = lax.broadcasted_iota(i32, full.shape, 0) % DG
    same = d == lax.broadcasted_iota(i32, full.shape, 1) % DG
    return jnp.where(same, full, 0.0).astype(bf16)


def spread_t(hidden):
    k, h = hidden.shape
    rows = lax.broadcasted_iota(i32, (h * DG, h), 0) // DG
    pick = (rows == lax.broadcasted_iota(i32, (h * DG, h), 1)).astype(bf16)
    tall = dot(pick, hidden, ((1,), (1,))).astype(bf16)
    columns = lax.broadcasted_iota(i32, (k, k * DG), 1) // DG
    widen = (columns == lax.broadcasted_iota(i32, (k, k * DG), 0)).astype(bf16)
    full = dot(tall, widen)
    d = lax.broadcasted_iota(i32, full.shape, 0) % DG
    same = d == lax.broadcasted_iota(i32, full.shape, 1) % DG
    return jnp.where(same, full, 0.0).astype(bf16)


def remote(src, dst, send, recv, dp, hyper):
    return pltpu.make_async_remote_copy(
        src_ref=src, dst_ref=dst, send_sem=send, recv_sem=recv, device_id={"dp": dp, "hyper": hyper}
    )


class Flood:
    def __init__(self, out, sems, n_dp, half):
        self.out, self.sems = out, sems
        self.na, self.half, self.n_hyper = n_dp // 2, half, 2 * half
        self.i, self.j, self.partner = place()
        self.a, self.b = self.i // 2, lax.rem(self.i, 2)
        self.cut = out.shape[2] // 32 * 16
        self.tall = out.shape[2]
        self.copies = {}

    @staticmethod
    def scratch(n_dp, half):
        dma, na = pltpu.SemaphoreType.DMA, n_dp // 2
        shapes = [(na,), (na,), (na, half), (na, half), (na, half), (na, 2, half)]
        return [dma(s) for s in shapes for _ in range(2)]

    def at(self, t, b, u):
        dp = source(self.a, t, self.na) * 2 + (self.b if b == 0 else 1 - self.b)
        return dp, lax.rem(self.j + self.n_hyper - 2 * u, self.n_hyper)

    def send(self, kind, index, block, where, dp, hyper, rows=None):
        number = "zxypqc".index(kind)
        s, r = self.sems[2 * number], self.sems[2 * number + 1]
        target = self.out.at[where[0], where[1]]
        if rows is not None:
            block, target = block.at[pl.ds(*rows)], target.at[pl.ds(*rows)]
        copy = remote(block, target, s.at[index], r.at[index], dp, hyper)
        copy.start()
        self.copies[kind, index] = copy

    def recv(self, kind, index):
        self.copies[kind, index].wait_recv()

    def peers(self):
        return [(u, lax.rem(self.j + 2 * u, self.n_hyper)) for u in range(1, self.half)]

    def column(self, t, own=None):
        where = self.at(t, 0, 0)
        if t:
            self.recv("z", (t,))
        block = self.out.at[where[0], where[1]] if own is None else own
        for u, peer in self.peers():
            self.send("y", (t, u), block, where, self.i, peer)
        self.send("x", (t,), block, where, self.a * 2 + 1 - self.b, self.j)
        self.send("c", (t, 0, 0), block, where, self.i, self.partner)

    def begin(self, own):
        where = self.at(0, 0, 0)
        for t in range(1, self.na):
            self.send("z", (t,), own, where, swap(self.a, t, self.na) * 2 + self.b, self.j)
        self.column(0, own)

    def pair(self, t):
        where = self.at(t, 1, 0)
        self.recv("x", (t,))
        block = self.out.at[where[0], where[1]]
        for u, peer in self.peers():
            self.send("p", (t, u), block, where, self.i, peer, (0, self.cut))
        self.send("c", (t, 1, 0), block, where, self.i, self.partner)

    def across(self, t):
        for u, peer in self.peers():
            where = self.at(t, 0, u)
            self.recv("y", (t, u))
            block = self.out.at[where[0], where[1]]
            self.send("c", (t, 0, u), block, where, self.i, self.partner)
            self.send(
                "q", (t, u), block, where, self.a * 2 + 1 - self.b, self.j, (self.cut, self.tall - self.cut)
            )

    def corner(self, t):
        for u, peer in self.peers():
            where = self.at(t, 1, u)
            self.recv("p", (t, u))
            self.recv("q", (t, u))
            self.send("c", (t, 1, u), self.out.at[where[0], where[1]], where, self.i, self.partner)

    def near(self, t):
        for u in range(self.half):
            self.recv("c", (t, 0, u))

    def far(self, t):
        for u in range(self.half):
            self.recv("c", (t, 1, u))

    def end(self):
        for copy in self.copies.values():
            copy.wait_send()


def hypernet(tiles, own, emb, hin_t, hb):
    blocks = tiles.shape[0]
    tiles = tiles.astype(f32)
    ids = (tiles[:, :8] * 256.0 + tiles[:, 8:]).reshape(blocks * 8, tiles.shape[2])[:, :1]
    clients = emb.shape[0]
    wide = (ids == lax.broadcasted_iota(i32, (blocks * 8, clients), 1).astype(f32)).astype(f32).astype(bf16)
    slots = blocks * own
    row = lax.broadcasted_iota(i32, (slots, blocks * 8), 0)
    column = lax.broadcasted_iota(i32, (slots, blocks * 8), 1)
    keep = (column == row // own * 8 + row % own).astype(f32).astype(bf16)
    select = dot(keep, wide).astype(bf16)
    picked = dot(select, emb).astype(bf16)
    preact = dot(picked, hin_t, ((1,), (1,))) + hb
    hidden = (preact / (1.0 + jnp.exp(-preact))).astype(bf16)
    return select, picked, preact, hidden


def main_kernel(
    n_dp, half, own, rows, aligned,
    x_ref, ids_ref, lab_ref, ew_ref, eb_ref, wn_ref, bn_ref, emb_ref, hin_ref, hb_ref, ho_ref,
    gw_all, dh_all, dheads_out, hid_out, pre_out, picked_out, select_out,
    packed, xg, dl_all, own_dl, w_wide, w_narrow, bufs, ho_n, diag_f, heads_f, part,
    from_partner, summed, from_peer, diag, heads, dheads, feats, slopes, dpre, total,
    gw_acc, gb_acc, gw_own, dh_mine, b1, b2, dh_sum, local_sems, buf_sems,
    sp, rp, sq, rq, sa, ra, sb, rb, sc, rc, *floods
):
    count = len(floods) // 3
    i, j, partner = place()
    n_hyper = 2 * half
    tall, width = x_ref.shape
    hh, wide, classes = ho_ref.shape
    chunk = bufs.shape[2]
    chunks = wide // chunk
    narrow = wide // n_dp
    groups = narrow // DG
    depth = bufs.shape[0]
    slots = n_dp * n_hyper * own
    group = n_hyper * own
    CS = diag.shape[0] // DG

    def buffer(c, slot):
        at = pl.ds(pl.multiple_of(c * chunk, chunk), chunk)
        return pltpu.make_async_copy(ho_ref.at[:, at, :], bufs.at[slot], buf_sems.at[slot])

    for c in range(min(depth, chunks)):
        buffer(c, c).start()
    wide_at = pl.ds(pl.multiple_of(j * wide, 128), wide)
    get_w = pltpu.make_async_copy(ew_ref.at[:, wide_at], w_wide, local_sems.at[0])
    get_w.start()
    get_h = pltpu.make_async_copy(
        ho_ref.at[:, pl.ds(pl.multiple_of(i * narrow, narrow), narrow), :], ho_n, local_sems.at[1]
    )
    get_h.start()
    first = (j * n_dp + i) * narrow
    if aligned:
        narrow_at = pl.ds(pl.multiple_of(first, 128), narrow)
        get_n = pltpu.make_async_copy(ew_ref.at[:, narrow_at], w_narrow, local_sems.at[2])
        get_n.start()

    row = lax.broadcasted_iota(i32, (16, width), 0)
    tile = jnp.zeros((16, width), f32)
    for s in range(own):
        number = ids_ref[s]
        tile = jnp.where(row == s, (number // 256).astype(f32), tile)
        tile = jnp.where(row == 8 + s, (number % 256).astype(f32), tile)
    packed[:tall] = x_ref[...]
    packed[tall:] = tile.astype(bf16)
    xg[i, j, :tall] = x_ref[...]
    xg[i, j, tall:] = tile.astype(bf16)

    sem = pltpu.get_barrier_semaphore()
    others = [(swap(i, t, n_dp), j) for t in range(1, n_dp)]
    others += [(i, lax.rem(j + u, n_hyper)) for u in range(1, n_hyper)]
    for dp, hyper in others:
        pl.semaphore_signal(sem, 1, device_id={"dp": dp, "hyper": hyper})
    pl.semaphore_wait(sem, len(others))

    na = n_dp // 2
    inp = Flood(xg, floods[:count], n_dp, half)
    inp.begin(packed)
    inp.across(0)
    inp.near(0)
    small = (emb_ref[...], hin_ref[...], hb_ref[...])
    diag_f[...] = spread(hypernet(xg[i, :, tall:, :], own, *small)[3])
    part[...] = jnp.zeros_like(part)
    get_w.wait()

    def forward(c, carry):
        slot = lax.rem(c, depth)
        buffer(c, slot).wait()
        for g in range(chunk // DG):
            rhs = bufs[slot, :, g * DG : (g + 1) * DG, :].reshape(hh * DG, classes)
            out = dot(diag_f[...], rhs).astype(bf16)
            heads_f[:, g * DG : (g + 1) * DG, :] = out.reshape(group, DG, classes)

        @pl.when(c + depth < chunks)
        def _():
            buffer(c + depth, slot).start()

        w = w_wide[:, pl.ds(pl.multiple_of(c * chunk, chunk), chunk)]
        bias = eb_ref[:, pl.ds(pl.multiple_of(j * wide + c * chunk, chunk), chunk)].astype(f32)
        for p in range(n_hyper):
            pre = dot(xg[i, p, :tall, :], w) + bias
            feat = (pre / (1.0 + jnp.exp(-pre))).astype(bf16)
            for s in range(own):
                part[p, s * rows : (s + 1) * rows, :] += dot(feat[s * rows : (s + 1) * rows], heads_f[p * own + s])
        return carry

    lax.fori_loop(0, chunks // 2, forward, 0)
    for t in range(1, na):
        inp.column(t)
    inp.pair(0)
    lax.fori_loop(chunks // 2, chunks, forward, 0)
    for t in range(1, na):
        inp.pair(t)
        inp.across(t)
    inp.corner(0)

    to_partner = {}
    for u in list(range(1, half)) + [0]:
        to_partner[u] = remote(
            part.at[lax.rem(partner + 2 * u, n_hyper)], from_partner.at[u], sp.at[u], rp.at[u], i, partner
        )
        to_partner[u].start()
    to_peer = {}
    for u in range(1, half):
        peer = lax.rem(j + 2 * u, n_hyper)
        to_partner[u].wait_recv()
        summed[u] = part[peer] + from_partner[u]
        to_peer[u] = remote(summed.at[u], from_peer.at[u], sq.at[u], rq.at[u], i, peer)
        to_peer[u].start()
    for t in range(1, na):
        inp.corner(t)
        inp.near(t)
    for t in range(na):
        inp.far(t)
    tiles = xg[:, :, tall:, :].reshape(n_dp * n_hyper, 16, width)
    select, picked, preact, hidden = hypernet(tiles, own, *small)
    select_out[...] = select
    picked_out[...] = picked
    pre_out[...] = preact
    hid_out[...] = hidden
    if aligned:
        get_n.wait()
        bias_n = eb_ref[:, pl.ds(pl.multiple_of(first, 128), narrow)].astype(f32)
        w_n = w_narrow
    else:
        bias_n = bn_ref[...].astype(f32)
        w_n = wn_ref

    nq = CS // group

    def prepare(base):
        mine = hid_out[pl.ds(pl.multiple_of(base * group, group), CS), :]
        diag[...] = spread(mine)

        def features(q, carry):
            for p in range(n_hyper):
                pre = dot(xg[base + q, p, :tall, :], w_n[...]) + bias_n
                logistic = 1.0 / (1.0 + jnp.exp(-pre))
                at = pl.ds(pl.multiple_of((q * n_hyper + p) * tall, tall), tall)
                feats[at, :] = (pre * logistic).astype(bf16)
                slopes[at, :] = logistic * (1.0 + pre * (1.0 - logistic))
            return carry

        lax.fori_loop(0, nq, features, 0)

    single = nq == n_dp
    if single:
        prepare(0)
    to_partner[0].wait_recv()
    logits = part[j] + from_partner[0]
    for u in range(1, half):
        to_peer[u].wait_recv()
        logits = logits + from_peer[u]
    eye = lax.broadcasted_iota(i32, (rows, rows), 0) == lax.broadcasted_iota(i32, (rows, rows), 1)
    columns = []
    for s in range(own):
        spot = jnp.where(eye, lab_ref[s : s + 1, :], 0)
        columns.append(jnp.sum(spot, axis=1, keepdims=True))
    label = jnp.concatenate(columns, axis=0)
    largest = jnp.max(logits, axis=-1, keepdims=True)
    exponent = jnp.exp(logits - largest)
    probability = exponent / jnp.sum(exponent, axis=-1, keepdims=True)
    onehot = (label == lax.broadcasted_iota(i32, logits.shape, 1)).astype(f32)
    dl = ((probability - onehot) / rows).astype(bf16)
    own_dl[...] = dl
    dl_all[i, j] = dl
    grads = Flood(dl_all, floods[count : 2 * count], n_dp, half)
    grads.begin(own_dl)

    gw_acc[...] = jnp.zeros_like(gw_acc)
    gb_acc[...] = jnp.zeros_like(gb_acc)

    def ho_group(g):
        return ho_n[:, pl.ds(pl.multiple_of(g * DG, DG), DG), :].reshape(hh * DG, classes)

    def heads_part(low, high):
        def step(g, carry):
            out = dot(diag[...], ho_group(g)).astype(bf16)
            heads[:, pl.ds(pl.multiple_of(g * DG, DG), DG), :] = out.reshape(CS, DG, classes)
            return carry

        lax.fori_loop(low, high, step, 0)

    def slots_part(base, low):
        def step(n, carry):
            q = low + n
            gw, gb = gw_acc[...], gb_acc[...]
            for p in range(n_hyper):
                block = (q - base) * n_hyper + p
                for s in range(own):
                    dl_s = dl_all[q, p, s * rows : (s + 1) * rows, :]
                    at = pl.ds(pl.multiple_of(block * tall + s * rows, rows), rows)
                    slot = (q * n_hyper + p) * own + s
                    dhead = dot(feats[at, :], dl_s, ((0,), (0,))).astype(bf16)
                    dheads[:, pl.ds(pl.multiple_of(slot * DG, DG), DG), :] = dhead.reshape(groups, DG, classes)
                    dfeat = dot(dl_s, heads[block * own + s], ((1,), (1,))).astype(bf16)
                    dpre[at, :] = (dfeat.astype(f32) * slopes[at, :]).astype(bf16)
            for p in range(n_hyper):
                block = (q - base) * n_hyper + p
                both = dpre[pl.ds(pl.multiple_of(block * tall, tall), tall), :]
                gw = gw + dot(xg[q, p, :tall, :], both, ((0,), (0,)))
                gb = gb + jnp.sum(both.astype(f32), axis=0, keepdims=True)
            gw_acc[...], gb_acc[...] = gw, gb
            return carry

        lax.fori_loop(0, 2, step, 0)

    def total_part(base, low, high):
        def step(g, carry):
            block = dheads[g, pl.ds(pl.multiple_of(base * group * DG, group * DG), CS * DG), :]
            total[...] += dot(block, ho_group(g), ((1,), (1,)))
            return carry

        lax.fori_loop(low, high, step, 0)

    def total_end(base):
        d = lax.broadcasted_iota(i32, total.shape, 0) % DG
        same = d == lax.broadcasted_iota(i32, total.shape, 1) % DG
        kept = jnp.sum(jnp.where(same, total[...], 0.0).reshape(CS, DG, hh * DG), axis=1)
        columns = lax.broadcasted_iota(i32, (hh * DG, 128), 0) // DG
        fold = (columns == lax.broadcasted_iota(i32, (hh * DG, 128), 1)).astype(f32)
        dh_mine[pl.ds(pl.multiple_of(base * group, group), CS), :] = dot(kept, fold, precision=highest)

    def flood_first(flood, work, count):
        cuts = [count * (t + 1) // na for t in range(na)]
        done = 0
        for t in range(1, na):
            work(done, cuts[t - 1])
            done = cuts[t - 1]
            flood.column(t)
            flood.pair(t - 1)
            flood.across(t - 1)
        flood.corner(0)
        work(done, count)
        flood.pair(na - 1)
        flood.across(na - 1)

    get_h.wait()
    if single:
        flood_first(grads, heads_part, groups)
        for t in range(na):
            if t + 1 < na:
                grads.corner(t + 1)
            grads.near(t)
            grads.far(t)
            slots_part(0, source(grads.a, t, na) * 2)
    else:
        flood_first(grads, lambda low, high: None, groups)
        for t in range(na):
            if t + 1 < na:
                grads.corner(t + 1)
            grads.near(t)
            grads.far(t)

        def one(q, carry):
            prepare(q * nq)
            heads_part(0, groups)
            for n in range(nq // 2):
                slots_part(q * nq, q * nq + 2 * n)
            total[...] = jnp.zeros_like(total)
            total_part(q * nq, 0, groups)
            total_end(q * nq)
            return carry

        lax.fori_loop(0, n_dp // nq, one, 0)
    put_heads = pltpu.make_async_copy(dheads, dheads_out, local_sems.at[3])
    put_heads.start()
    gw_own[:width] = gw_acc[...].astype(bf16)
    gw_own[width:] = jnp.broadcast_to(gb_acc[...], (16, narrow)).astype(bf16)
    if aligned:
        gw_all[i, j] = gw_own[...]
    else:
        put_own = pltpu.make_async_copy(gw_own, gw_all.at[i, j], local_sems.at[2])
        put_own.start()
        put_own.wait()
    fin = Flood(gw_all, floods[2 * count :], n_dp, half)
    fin.begin(gw_own)
    if single:
        total[...] = jnp.zeros_like(total)
        flood_first(fin, functools.partial(total_part, 0), groups)
        total_end(0)
    else:
        flood_first(fin, lambda low, high: None, groups)

    share = slots // n_hyper
    peers = [lax.rem(j + u, n_hyper) for u in range(1, n_hyper)]
    to_hyper = []
    for u in range(1, n_hyper):
        at = pl.ds(pl.multiple_of(peers[u - 1] * share, share), share)
        copy = remote(dh_mine.at[at], b1.at[u], sa.at[u], ra.at[u], i, peers[u - 1])
        copy.start()
        to_hyper.append(copy)
    for t in range(1, na):
        fin.corner(t)
    quarter = dh_mine[pl.ds(pl.multiple_of(j * share, share), share), :]
    for u in range(1, n_hyper):
        to_hyper[u - 1].wait_recv()
        quarter = quarter + b1[u]
    dh_sum[0] = quarter
    b2[i] = quarter
    to_dp = []
    for t in range(1, n_dp):
        copy = remote(dh_sum.at[0], b2.at[i], sb.at[t], rb.at[t], swap(i, t, n_dp), j)
        copy.start()
        to_dp.append(copy)
    for t in range(na):
        fin.near(t)
        fin.far(t)
    for copy in to_dp:
        copy.wait_recv()
    sum_all = b2[0]
    for t in range(1, n_dp):
        sum_all = sum_all + b2[t]
    dh_sum[1] = sum_all
    dh_all[j] = sum_all
    last = []
    for u in range(1, n_hyper):
        copy = remote(dh_sum.at[1], dh_all.at[j], sc.at[u], rc.at[u], i, peers[u - 1])
        copy.start()
        last.append(copy)
    for copy in last:
        copy.wait_recv()
    put_heads.wait()
    for copy in list(to_partner.values()) + list(to_peer.values()) + to_hyper + to_dp + last:
        copy.wait_send()
    for flood in (inp, grads, fin):
        flood.end()


def main_part(x, ids, labels, ew, eb, wn, bn, emb, hin_t, hb, ho, n_dp, n_hyper, aligned):
    own, rows = labels.shape
    tall, width = x.shape
    hh, wide, classes = ho.shape
    narrow = wide // n_dp
    half = n_hyper // 2
    group = n_hyper * own
    slots = group * n_dp
    CS = slots if slots <= 64 else 2 * group
    chunk = 128
    depth = 3 if slots <= 64 else 2
    block = tall + 16
    share = slots // n_hyper
    dma = pltpu.SemaphoreType.DMA
    sample = CS * rows
    vm = pltpu.VMEM
    ANY = pl.BlockSpec(memory_space=pl.ANY)
    shape = jax.ShapeDtypeStruct
    return pl.pallas_call(
        functools.partial(main_kernel, n_dp, half, own, rows, aligned),
        out_shape=(
            shape((n_dp, n_hyper, width + 16, narrow), bf16),
            shape((n_hyper, share, 128), f32),
            shape((narrow // DG, slots * DG, classes), bf16),
            shape((slots, hh), bf16),
            shape((slots, hh), f32),
            shape((slots, emb.shape[1]), bf16),
            shape((slots, emb.shape[0]), bf16),
        ),
        in_specs=[VM, pl.BlockSpec(memory_space=pltpu.SMEM), VM, ANY, VM, VM, VM, VM, VM, VM, ANY],
        out_specs=(VM if aligned else ANY, VM, ANY, VM, VM, VM, VM),
        scratch_shapes=[
            vm((block, width), bf16),
            vm((n_dp, n_hyper, block, width), bf16),
            vm((n_dp, n_hyper, tall, classes), bf16),
            vm((tall, classes), bf16),
            vm((width, wide), bf16),
            vm((width, narrow), bf16),
            vm((depth, hh, chunk, classes), bf16),
            vm((hh, narrow, classes), bf16),
            vm((group * DG, hh * DG), bf16),
            vm((group, chunk, classes), bf16),
            vm((n_hyper, tall, classes), f32),
            vm((half, tall, classes), f32),
            vm((half, tall, classes), f32),
            vm((half, tall, classes), f32),
            vm((CS * DG, hh * DG), bf16),
            vm((CS, narrow, classes), bf16),
            vm((narrow // DG, slots * DG, classes), bf16),
            vm((sample, narrow), bf16),
            vm((sample, narrow), f32),
            vm((sample, narrow), bf16),
            vm((CS * DG, hh * DG), f32),
            vm((width, narrow), f32),
            vm((1, narrow), f32),
            vm((width + 16, narrow), bf16),
            vm((slots, 128), f32),
            vm((n_hyper, share, 128), f32),
            vm((n_dp, share, 128), f32),
            vm((2, share, 128), f32),
            dma((4,)),
            dma((depth,)),
        ]
        + [dma((half,)) for _ in range(4)]
        + [dma((n_hyper,)), dma((n_hyper,)), dma((n_dp,)), dma((n_dp,)), dma((n_hyper,)), dma((n_hyper,))]
        + Flood.scratch(n_dp, half) * 3,
        compiler_params=pltpu.CompilerParams(
            collective_id=0, has_side_effects=True, vmem_limit_bytes=LIMIT
        ),
        name="main_part",
    )(x, ids, labels, ew, eb, wn, bn, emb, hin_t, hb, ho)


def last_kernel(aligned, dheads_ref, hid_ref, pre_ref, picked_ref, select_ref, hin_ref, dh_ref, gw_ref,
                go_ref, gwf_ref, gb_ref, table_ref, in_ref, hb_ref, diag_t):
    hh = go_ref.shape[0]
    classes = go_ref.shape[2]

    @pl.when(pl.program_id(0) == 0)
    def _():
        diag_t[...] = spread_t(hid_ref[...])
        dpre = dh_ref[...][:, :hh] * silu_slope(pre_ref[...])
        hb_ref[...] = jnp.sum(dpre, axis=0, keepdims=True)
        in_ref[...] = dot(dpre, picked_ref[...].astype(f32), ((0,), (0,)), precision=highest)
        back = dot(dpre, hin_ref[...].astype(f32), precision=highest)
        table_ref[...] = dot(select_ref[...].astype(f32), back, ((0,), (0,)), precision=highest)
        if aligned:
            n_dp, n_hyper, tall, narrow = gw_ref.shape
            for jj in range(n_hyper):
                for ii in range(n_dp):
                    at = (jj * n_dp + ii) * narrow
                    gwf_ref[:, at : at + narrow] = gw_ref[ii, jj, : tall - 16, :].astype(f32)
                    gb_ref[:, at : at + narrow] = gw_ref[ii, jj, tall - 16 : tall - 8, :].astype(f32)[:1]

    go_ref[...] = dot(diag_t[...], dheads_ref[0]).reshape(hh, DG, classes)


def last_part(dheads, hid, pre, picked, select, hin_t, dh, gw_all, aligned):
    groups, tall, classes = dheads.shape
    slots, hh = hid.shape
    width = picked.shape[1]
    clients = select.shape[1]
    n_dp, n_hyper, block, narrow = gw_all.shape
    whole = lambda *s: pl.BlockSpec(s, lambda g: (0,) * len(s))
    shape = jax.ShapeDtypeStruct
    full = (block - 16, n_dp * n_hyper * narrow) if aligned else (8, 128)
    bias = (1, full[1])
    given = gw_all if aligned else gw_all[:1, :1]
    return pl.pallas_call(
        functools.partial(last_kernel, aligned),
        grid=(groups,),
        out_shape=(
            shape((hh, groups * DG, classes), f32),
            shape(full, f32),
            shape(bias, f32),
            shape((clients, hin_t.shape[1]), f32),
            shape((hh, width), f32),
            shape((1, hh), f32),
        ),
        in_specs=[
            pl.BlockSpec((1, tall, classes), lambda g: (g, 0, 0)),
            whole(slots, hh), whole(slots, hh), whole(slots, width), whole(slots, clients),
            whole(*hin_t.shape), whole(slots, 128), whole(*given.shape),
        ],
        out_specs=[
            pl.BlockSpec((hh, DG, classes), lambda g: (0, g, 0)),
            whole(*full), whole(*bias), whole(clients, hin_t.shape[1]), whole(hh, width), whole(1, hh),
        ],
        scratch_shapes=[pltpu.VMEM((hh * DG, slots * DG), bf16)],
        compiler_params=pltpu.CompilerParams(vmem_limit_bytes=LIMIT),
        name="last_part",
    )(dheads, hid, pre, picked, select, hin_t, dh, given)


def local(
    inputs, labels, client_ids, ext_weight, ext_bias, embeddings, hyper_in, hyper_bias, hyper_out
):
    n_dp, n_hyper = lax.axis_size("dp"), lax.axis_size("hyper")
    own, rows, width = inputs.shape
    narrow = hyper_out.shape[0] // n_dp
    aligned = narrow % 128 == 0
    ho = hyper_out.transpose(1, 0, 2)
    hin_t = hyper_in.T
    bias = ext_bias[None]
    if aligned:
        wn, bn = jnp.zeros((8, 128), bf16), jnp.zeros((1, 128), bf16)
    else:
        start = (lax.axis_index("hyper") * n_dp + lax.axis_index("dp")) * narrow
        wn = lax.dynamic_slice_in_dim(ext_weight, start, narrow, 1)
        bn = lax.dynamic_slice_in_dim(bias, start, narrow, 1)
    gw_all, dh, dheads, hid, pre, picked, select = main_part(
        inputs.reshape(own * rows, width), client_ids, labels, ext_weight, bias, wn, bn,
        embeddings, hin_t, hyper_bias[None], ho, n_dp, n_hyper, aligned,
    )
    grad_out, gw, gb, table, grad_in, grad_hb = last_part(
        dheads, hid, pre, picked, select, hin_t, dh.reshape(-1, 128), gw_all, aligned
    )
    if not aligned:
        gw = gw_all[:, :, :width].transpose(2, 1, 0, 3).reshape(width, -1).astype(f32)
        gb = gw_all[:, :, width].transpose(1, 0, 2).reshape(-1).astype(f32)
    return (gw, gb.reshape(-1), table, grad_in.T, grad_hb.reshape(-1), grad_out.transpose(1, 0, 2))


def solution(mesh):
    placed = (
        P(("dp", "hyper"), None, None),
        P(("dp", "hyper"), None),
        P(("dp", "hyper")),
        P(),
        P(),
        P(),
        P(),
        P(),
        P("hyper", None, None),
    )
    return jax.shard_map(
        local,
        mesh=mesh,
        in_specs=placed,
        out_specs=(P(), P(), P(), P(), P(), P(("hyper", "dp"), None, None)),
        check_vma=False,
    )
```

time: 213 us -> 88.6 us (0.42)
  Pallas kernels: 0 us -> 84.9 us
  matrix products: 63.2 us -> 0 us
  blocking collectives: 58.7 us -> 0 us
  waiting for transfers between devices: 44.1 us -> 0 us
  local copies, waits for them, and re-layouts: 27.1 us -> 2.4 us
  between operations: 13.9 us -> 0.8 us
  other arithmetic: 5.5 us -> 0 us
    pallas_call x0 -> x2, Pallas kernels: none -> 84.9 us  [the longest x1 73.6 us: main_part(): pl.pallas_call(functools.partial(main_kernel, n_dp, half, own, rows, alig...]
    dot_general x16 -> x0, matrix products: 63.2 us -> none  [the longest x1 29.1 us: local(): jnp.einsum('kh,dhc->kdc', hidden_group, hyper_out, preferred_element_type...]
    all_gather x3 -> x0, waiting for transfers between devices: 44.1 us -> none  [the longest x1 44.1 us: local(): dl_all = lax.all_gather(dlogits, everyone, axis=0, tiled=True)]
    psum x1 -> x0, blocking collectives: 39.9 us -> none  [local(): dhidden, bias_rows = lax.psum((dhidden, bias_rows), everyone)]
    all_to_all x1 -> x0, blocking collectives: 11.7 us -> none  [local(): lax.all_to_all(part.reshape(n_hyper, own * rows, classes), 'hyper', split...]
    unnamed x24 -> x0, local copies, waits for them, and re-layouts: 9.45 us -> none
    all_gather x1 -> x0, blocking collectives: 7.06 us -> none  [local(): from_group = lax.all_gather(packed, 'hyper', axis=0)]
    convert_element_type x1 -> x0, local copies, waits for them, and re-layouts: 6.61 us -> none  [local(): jnp.einsum('krd,krc->kdc', features, dl_all, preferred_element_type=f32)]
  transfers between devices with their start and end apart: 3 -> 0, of which waited for: 1 -> 0; matrix products, arithmetic and copies ran while one was open for 38% -> 0% of each run, Pallas kernels for 0% -> 0%
where the time goes in v2:
time: 88.6 us; the launch traced here: 88.2 us
  Pallas kernels  84.9 us (96%)
  local copies, waits for them, and re-layouts  2.4 us (3%)
    pallas_call x1, Pallas kernels, main_part(): pl.pallas_call(functools.partial(main_kernel, n_dp, half, own, rows, alig...  73.6 us
    pallas_call x1, Pallas kernels, last_part(): pl.pallas_call(functools.partial(last_kernel, aligned), grid=(groups,), o...  11.4 us

profile of v2, /device:TPU:0, one launch (start us, length us, event | category | flops | bytes accessed | tf_op | source)
XLA Modules:
  0.0 88.2 jit_solution(567555305889540383)
XLA Ops:
  0.6 1.3 %broadcast_in_dim.12.eb_ref = bf16[1,4096]{1,0:T(2,128)(2,1)} reshape(bf16[4096]{0:T(1024)(128)(2,1)} %param.13) | data formatting | bytes 16384 | tf_op jit(solution)/shard_map/broadcast_in_dim | solution.py:667
  1.9 0.5 broadcast_in_dim.14.bn_ref
  2.5 0.6 broadcast_in_dim.13.wn_ref
  3.0 73.6 %main_part.1 = (bf16[8,4,144,128]{3,2,1,0:T(8,128)(2,1)}, f32[4,16,128]{2,1,0:T(8,128)}, bf16[8,1024,256]{2,1,0:T(8,128)(2,1)}, bf16[64,50]{1,0:T(8,128)(2,1)}, ...) custom-call(bf16[128,128]{1,0:T(8,128)(2,1)} %bitcast.12, s32[2]{0:T(128)} %ids_ref.1, ...), custom_call_target="tpu_custom_call" | custom-call | tf_op jit(solution)/shard_map/main_part/pallas_call | solution.py:542
  76.6 11.4 %last_part.1 = (f32[50,128,256]{2,1,0:T(8,128)}, f32[128,4096]{1,0:T(8,128)}, f32[1,4096]{1,0:T(1,128)}, f32[64,128]{1,0:T(8,128)}, f32[50,128]{1,0:T(8,128)}, /*index=5*/f32[1,50]{1,0:T(1,128)}) custom-call(bf16[8,1024,256]{2,1,0:T(8,128)(2,1)} %get-tuple-element.19.dheads_ref, bf16[64,50]{1,0:T(8,128)(2,1)} %get-tuple-element.20.hid_ref, ...), custom_call_target="tpu_custom_call" | custom-call | tf_op jit(solution)/shard_map/last_part/pallas_call | solution.py:632

commit v3 on v2

--- a/solution.py
+++ b/solution.py
@@ -190,11 +190,11 @@
 def main_kernel(
     n_dp, half, own, rows, aligned,
     x_ref, ids_ref, lab_ref, ew_ref, eb_ref, wn_ref, bn_ref, emb_ref, hin_ref, hb_ref, ho_ref,
-    gw_all, dh_all, dheads_out, hid_out, pre_out, picked_out, select_out,
+    gw_all, dh_all, go_out, pre_out, picked_out, select_out,
     packed, xg, dl_all, own_dl, w_wide, w_narrow, bufs, ho_n, diag_f, heads_f, part,
-    from_partner, summed, from_peer, diag, heads, dheads, feats, slopes, dpre, total,
-    gw_acc, gb_acc, gw_own, dh_mine, b1, b2, dh_sum, local_sems, buf_sems,
-    sp, rp, sq, rq, sa, ra, sb, rb, sc, rc, *floods
+    from_partner, summed, from_peer, diag, heads, dheads, diag_t, go, go_acc, feats, slopes, dpre,
+    gw_acc, gb_acc, gw_own, dh_mine, b1, b2, dh_sum, hid_out, bias_w, id_own, id_all, local_sems, buf_sems,
+    sp, rp, sq, rq, si, ri, sa, ra, sb, rb, sc, rc, *floods
 ):
     count = len(floods) // 3
     i, j, partner = place()
@@ -237,6 +237,8 @@
         tile = jnp.where(row == 8 + s, (number % 256).astype(f32), tile)
     packed[:tall] = x_ref[...]
     packed[tall:] = tile.astype(bf16)
+    id_own[...] = tile.astype(bf16)
+    id_all[j] = tile.astype(bf16)
     xg[i, j, :tall] = x_ref[...]
     xg[i, j, tall:] = tile.astype(bf16)
 
@@ -249,13 +251,21 @@
 
     na = n_dp // 2
     inp = Flood(xg, floods[:count], n_dp, half)
+    to_ids = []
+    for u in range(1, n_hyper):
+        copy = remote(id_own, id_all.at[j], si.at[u], ri.at[u], i, lax.rem(j + u, n_hyper))
+        copy.start()
+        to_ids.append(copy)
     inp.begin(packed)
+    for copy in to_ids:
+        copy.wait_recv()
+    small = (emb_ref[...], hin_ref[...], hb_ref[...])
+    diag_f[...] = spread(hypernet(id_all[...], own, *small)[3])
+    part[...] = jnp.zeros_like(part)
+    bias_w[...] = eb_ref[pl.ds(pl.multiple_of(j * wide, 256), wide)].astype(f32)[None]
+    get_w.wait()
     inp.across(0)
     inp.near(0)
-    small = (emb_ref[...], hin_ref[...], hb_ref[...])
-    diag_f[...] = spread(hypernet(xg[i, :, tall:, :], own, *small)[3])
-    part[...] = jnp.zeros_like(part)
-    get_w.wait()
 
     def forward(c, carry):
         slot = lax.rem(c, depth)
@@ -270,7 +280,7 @@
             buffer(c + depth, slot).start()
 
         w = w_wide[:, pl.ds(pl.multiple_of(c * chunk, chunk), chunk)]
-        bias = eb_ref[:, pl.ds(pl.multiple_of(j * wide + c * chunk, chunk), chunk)].astype(f32)
+        bias = bias_w[:, pl.ds(pl.multiple_of(c * chunk, chunk), chunk)]
         for p in range(n_hyper):
             pre = dot(xg[i, p, :tall, :], w) + bias
             feat = (pre / (1.0 + jnp.exp(-pre))).astype(bf16)
@@ -314,7 +324,7 @@
     hid_out[...] = hidden
     if aligned:
         get_n.wait()
-        bias_n = eb_ref[:, pl.ds(pl.multiple_of(first, 128), narrow)].astype(f32)
+        bias_n = bias_w[:, pl.ds(pl.multiple_of(i * narrow, 128), narrow)]
         w_n = w_narrow
     else:
         bias_n = bn_ref[...].astype(f32)
@@ -340,6 +350,7 @@
     single = nq == n_dp
     if single:
         prepare(0)
+        diag_t[...] = spread_t(hidden)
     to_partner[0].wait_recv()
     logits = part[j] + from_partner[0]
     for u in range(1, half):
@@ -399,21 +410,29 @@
 
         lax.fori_loop(0, 2, step, 0)
 
-    def total_part(base, low, high):
+    def go_part(low, high):
         def step(g, carry):
-            block = dheads[g, pl.ds(pl.multiple_of(base * group * DG, group * DG), CS * DG), :]
-            total[...] += dot(block, ho_group(g), ((1,), (1,)))
+            at = pl.ds(pl.multiple_of(g * DG, DG), DG)
+            go[:, at, :] = dot(diag_t[...], dheads[g]).astype(bf16).reshape(hh, DG, classes)
             return carry
 
-        lax.fori_loop(low, high, step, 0)
-
-    def total_end(base):
-        d = lax.broadcasted_iota(i32, total.shape, 0) % DG
-        same = d == lax.broadcasted_iota(i32, total.shape, 1) % DG
-        kept = jnp.sum(jnp.where(same, total[...], 0.0).reshape(CS, DG, hh * DG), axis=1)
-        columns = lax.broadcasted_iota(i32, (hh * DG, 128), 0) // DG
-        fold = (columns == lax.broadcasted_iota(i32, (hh * DG, 128), 1)).astype(f32)
-        dh_mine[pl.ds(pl.multiple_of(base * group, group), CS), :] = dot(kept, fold, precision=highest)
+        if single:
+            lax.fori_loop(low, high, step, 0)
+
+    def total_part(q0):
+        count = 2 * group * DG
+        at = pl.ds(pl.multiple_of(q0 * group * DG, group * DG), count)
+        z = dot(ho_group(0), dheads[0, at, :], ((1,), (1,)))
+        for g in range(1, groups):
+            z = z + dot(ho_group(g), dheads[g, at, :], ((1,), (1,)))
+        d = lax.broadcasted_iota(i32, z.shape, 0) % DG
+        same = d == lax.broadcasted_iota(i32, z.shape, 1) % DG
+        kept = jnp.sum(jnp.where(same, z, 0.0).reshape(hh, DG, count), axis=1)
+        kept = jnp.concatenate([kept, jnp.zeros((128 - hh, count), f32)], axis=0)
+        fold = lax.broadcasted_iota(i32, (2 * group, count), 1) // DG
+        fold = (fold == lax.broadcasted_iota(i32, (2 * group, count), 0)).astype(f32)
+        mine = dot(fold, kept, ((1,), (1,)), precision=highest)
+        dh_mine[pl.ds(pl.multiple_of(q0 * group, group), 2 * group), :] = mine
 
     def flood_first(flood, work, count):
         cuts = [count * (t + 1) // na for t in range(na)]
@@ -438,6 +457,8 @@
             grads.near(t)
             grads.far(t)
             slots_part(0, source(grads.a, t, na) * 2)
+            if t + 1 < na:
+                total_part(source(grads.a, t, na) * 2)
     else:
         flood_first(grads, lambda low, high: None, groups)
         for t in range(na):
@@ -451,14 +472,19 @@
             heads_part(0, groups)
             for n in range(nq // 2):
                 slots_part(q * nq, q * nq + 2 * n)
-            total[...] = jnp.zeros_like(total)
-            total_part(q * nq, 0, groups)
-            total_end(q * nq)
+            for n in range(nq // 2):
+                total_part(q * nq + 2 * n)
+            diag_t[...] = spread_t(hid_out[pl.ds(pl.multiple_of(q * CS, CS), CS), :])
+            at = pl.ds(pl.multiple_of(q * CS * DG, CS * DG), CS * DG)
+            for g in range(groups):
+                spot = slice(g * DG, (g + 1) * DG)
+                go_acc[:, spot, :] += dot(diag_t[...], dheads[g, at, :]).reshape(hh, DG, classes)
             return carry
 
+        go_acc[...] = jnp.zeros_like(go_acc)
+
         lax.fori_loop(0, n_dp // nq, one, 0)
-    put_heads = pltpu.make_async_copy(dheads, dheads_out, local_sems.at[3])
-    put_heads.start()
+        go[...] = go_acc[...].astype(bf16)
     gw_own[:width] = gw_acc[...].astype(bf16)
     gw_own[width:] = jnp.broadcast_to(gb_acc[...], (16, narrow)).astype(bf16)
     if aligned:
@@ -470,11 +496,7 @@
     fin = Flood(gw_all, floods[2 * count :], n_dp, half)
     fin.begin(gw_own)
     if single:
-        total[...] = jnp.zeros_like(total)
-        flood_first(fin, functools.partial(total_part, 0), groups)
-        total_end(0)
-    else:
-        flood_first(fin, lambda low, high: None, groups)
+        total_part(source(grads.a, na - 1, na) * 2)
 
     share = slots // n_hyper
     peers = [lax.rem(j + u, n_hyper) for u in range(1, n_hyper)]
@@ -484,8 +506,11 @@
         copy = remote(dh_mine.at[at], b1.at[u], sa.at[u], ra.at[u], i, peers[u - 1])
         copy.start()
         to_hyper.append(copy)
-    for t in range(1, na):
-        fin.corner(t)
+    quart = groups // 4
+    go_part(0, quart)
+    fin.column(1)
+    fin.pair(0)
+    fin.across(0)
     quarter = dh_mine[pl.ds(pl.multiple_of(j * share, share), share), :]
     for u in range(1, n_hyper):
         to_hyper[u - 1].wait_recv()
@@ -497,9 +522,13 @@
         copy = remote(dh_sum.at[0], b2.at[i], sb.at[t], rb.at[t], swap(i, t, n_dp), j)
         copy.start()
         to_dp.append(copy)
-    for t in range(na):
-        fin.near(t)
-        fin.far(t)
+    go_part(quart, 2 * quart)
+    for t in range(2, na):
+        fin.column(t)
+        fin.pair(t - 1)
+        fin.across(t - 1)
+    fin.corner(0)
+    go_part(2 * quart, 3 * quart)
     for copy in to_dp:
         copy.wait_recv()
     sum_all = b2[0]
@@ -512,10 +541,20 @@
         copy = remote(dh_sum.at[1], dh_all.at[j], sc.at[u], rc.at[u], i, peers[u - 1])
         copy.start()
         last.append(copy)
+    fin.pair(na - 1)
+    fin.across(na - 1)
+    go_part(3 * quart, groups)
+    put_go = pltpu.make_async_copy(go, go_out, local_sems.at[3])
+    put_go.start()
+    for t in range(1, na):
+        fin.corner(t)
+    for t in range(na):
+        fin.near(t)
+        fin.far(t)
     for copy in last:
         copy.wait_recv()
-    put_heads.wait()
-    for copy in list(to_partner.values()) + list(to_peer.values()) + to_hyper + to_dp + last:
+    put_go.wait()
+    for copy in list(to_partner.values()) + list(to_peer.values()) + to_hyper + to_dp + last + to_ids:
         copy.wait_send()
     for flood in (inp, grads, fin):
         flood.end()
@@ -544,14 +583,13 @@
         out_shape=(
             shape((n_dp, n_hyper, width + 16, narrow), bf16),
             shape((n_hyper, share, 128), f32),
-            shape((narrow // DG, slots * DG, classes), bf16),
-            shape((slots, hh), bf16),
+            shape((hh, narrow, classes), bf16),
             shape((slots, hh), f32),
             shape((slots, emb.shape[1]), bf16),
             shape((slots, emb.shape[0]), bf16),
         ),
         in_specs=[VM, pl.BlockSpec(memory_space=pltpu.SMEM), VM, ANY, VM, VM, VM, VM, VM, VM, ANY],
-        out_specs=(VM if aligned else ANY, VM, ANY, VM, VM, VM, VM),
+        out_specs=(VM if aligned else ANY, VM, ANY, VM, VM, VM),
         scratch_shapes=[
             vm((block, width), bf16),
             vm((n_dp, n_hyper, block, width), bf16),
@@ -570,10 +608,12 @@
             vm((CS * DG, hh * DG), bf16),
             vm((CS, narrow, classes), bf16),
             vm((narrow // DG, slots * DG, classes), bf16),
+            vm((hh * DG, CS * DG), bf16),
+            vm((hh, narrow, classes), bf16),
+            vm((8, 8, 128) if CS == slots else (hh, narrow, classes), f32),
             vm((sample, narrow), bf16),
             vm((sample, narrow), f32),
             vm((sample, narrow), bf16),
-            vm((CS * DG, hh * DG), f32),
             vm((width, narrow), f32),
             vm((1, narrow), f32),
             vm((width + 16, narrow), bf16),
@@ -581,10 +621,15 @@
             vm((n_hyper, share, 128), f32),
             vm((n_dp, share, 128), f32),
             vm((2, share, 128), f32),
+            vm((slots, hh), bf16),
+            vm((1, wide), f32),
+            vm((16, width), bf16),
+            vm((n_hyper, 16, width), bf16),
             dma((4,)),
             dma((depth,)),
         ]
         + [dma((half,)) for _ in range(4)]
+        + [dma((n_hyper,)), dma((n_hyper,))]
         + [dma((n_hyper,)), dma((n_hyper,)), dma((n_dp,)), dma((n_dp,)), dma((n_hyper,)), dma((n_hyper,))]
         + Flood.scratch(n_dp, half) * 3,
         compiler_params=pltpu.CompilerParams(
@@ -594,19 +639,13 @@
     )(x, ids, labels, ew, eb, wn, bn, emb, hin_t, hb, ho)
 
 
-def last_kernel(aligned, dheads_ref, hid_ref, pre_ref, picked_ref, select_ref, hin_ref, dh_ref, gw_ref,
-                go_ref, gwf_ref, gb_ref, table_ref, in_ref, hb_ref, diag_t):
+def last_kernel(aligned, go_ref, pre_ref, picked_ref, select_ref, hin_ref, dh_ref, gw_ref,
+                go_out, gwf_out, gb_ref, table_ref, in_ref, hb_ref, gwf_ref, sem):
     hh = go_ref.shape[0]
-    classes = go_ref.shape[2]
-
-    @pl.when(pl.program_id(0) == 0)
+    last = pl.num_programs(0) - 1
+
+    @pl.when(pl.program_id(0) == jnp.minimum(1, last))
     def _():
-        diag_t[...] = spread_t(hid_ref[...])
-        dpre = dh_ref[...][:, :hh] * silu_slope(pre_ref[...])
-        hb_ref[...] = jnp.sum(dpre, axis=0, keepdims=True)
-        in_ref[...] = dot(dpre, picked_ref[...].astype(f32), ((0,), (0,)), precision=highest)
-        back = dot(dpre, hin_ref[...].astype(f32), precision=highest)
-        table_ref[...] = dot(select_ref[...].astype(f32), back, ((0,), (0,)), precision=highest)
         if aligned:
             n_dp, n_hyper, tall, narrow = gw_ref.shape
             for jj in range(n_hyper):
@@ -614,14 +653,27 @@
                     at = (jj * n_dp + ii) * narrow
                     gwf_ref[:, at : at + narrow] = gw_ref[ii, jj, : tall - 16, :].astype(f32)
                     gb_ref[:, at : at + narrow] = gw_ref[ii, jj, tall - 16 : tall - 8, :].astype(f32)[:1]
-
-    go_ref[...] = dot(diag_t[...], dheads_ref[0]).reshape(hh, DG, classes)
-
-
-def last_part(dheads, hid, pre, picked, select, hin_t, dh, gw_all, aligned):
-    groups, tall, classes = dheads.shape
-    slots, hh = hid.shape
-    width = picked.shape[1]
+            pltpu.make_async_copy(gwf_ref, gwf_out, sem).start()
+
+    @pl.when(pl.program_id(0) == jnp.minimum(2, last))
+    def _():
+        dpre = dh_ref[...][:, :hh] * silu_slope(pre_ref[...])
+        hb_ref[...] = jnp.sum(dpre, axis=0, keepdims=True)
+        in_ref[...] = dot(dpre, picked_ref[...].astype(f32), ((0,), (0,)), precision=highest)
+        back = dot(dpre, hin_ref[...].astype(f32), precision=highest)
+        table_ref[...] = dot(select_ref[...].astype(f32), back, ((0,), (0,)), precision=highest)
+
+    go_out[...] = go_ref[...].astype(f32)
+
+    @pl.when(pl.program_id(0) == last)
+    def _():
+        if aligned:
+            pltpu.make_async_copy(gwf_ref, gwf_out, sem).wait()
+
+
+def last_part(go, pre, picked, select, hin_t, dh, gw_all, aligned):
+    hh, wide, classes = go.shape
+    slots, width = picked.shape
     clients = select.shape[1]
     n_dp, n_hyper, block, narrow = gw_all.shape
     whole = lambda *s: pl.BlockSpec(s, lambda g: (0,) * len(s))
@@ -629,11 +681,13 @@
     full = (block - 16, n_dp * n_hyper * narrow) if aligned else (8, 128)
     bias = (1, full[1])
     given = gw_all if aligned else gw_all[:1, :1]
+    per = 32 if wide % 32 == 0 else wide
+    cut = pl.BlockSpec((hh, per, classes), lambda g: (0, g, 0))
     return pl.pallas_call(
         functools.partial(last_kernel, aligned),
-        grid=(groups,),
+        grid=(wide // per,),
         out_shape=(
-            shape((hh, groups * DG, classes), f32),
+            shape(go.shape, f32),
             shape(full, f32),
             shape(bias, f32),
             shape((clients, hin_t.shape[1]), f32),
@@ -641,18 +695,17 @@
             shape((1, hh), f32),
         ),
         in_specs=[
-            pl.BlockSpec((1, tall, classes), lambda g: (g, 0, 0)),
-            whole(slots, hh), whole(slots, hh), whole(slots, width), whole(slots, clients),
+            cut, whole(slots, hh), whole(slots, width), whole(slots, clients),
             whole(*hin_t.shape), whole(slots, 128), whole(*given.shape),
         ],
         out_specs=[
-            pl.BlockSpec((hh, DG, classes), lambda g: (0, g, 0)),
-            whole(*full), whole(*bias), whole(clients, hin_t.shape[1]), whole(hh, width), whole(1, hh),
+            cut, pl.BlockSpec(memory_space=pl.ANY),
+            whole(*bias), whole(clients, hin_t.shape[1]), whole(hh, width), whole(1, hh),
         ],
-        scratch_shapes=[pltpu.VMEM((hh * DG, slots * DG), bf16)],
+        scratch_shapes=[pltpu.VMEM(full, f32), pltpu.SemaphoreType.DMA],
         compiler_params=pltpu.CompilerParams(vmem_limit_bytes=LIMIT),
         name="last_part",
-    )(dheads, hid, pre, picked, select, hin_t, dh, given)
+    )(go, pre, picked, select, hin_t, dh, given)
 
 
 def local(
@@ -664,19 +717,19 @@
     aligned = narrow % 128 == 0
     ho = hyper_out.transpose(1, 0, 2)
     hin_t = hyper_in.T
-    bias = ext_bias[None]
+    bias = ext_bias
     if aligned:
-        wn, bn = jnp.zeros((8, 128), bf16), jnp.zeros((1, 128), bf16)
+        wn, bn = embeddings, hyper_bias[None]
     else:
         start = (lax.axis_index("hyper") * n_dp + lax.axis_index("dp")) * narrow
         wn = lax.dynamic_slice_in_dim(ext_weight, start, narrow, 1)
-        bn = lax.dynamic_slice_in_dim(bias, start, narrow, 1)
-    gw_all, dh, dheads, hid, pre, picked, select = main_part(
+        bn = lax.dynamic_slice_in_dim(bias, start, narrow, 0)[None]
+    gw_all, dh, go, pre, picked, select = main_part(
         inputs.reshape(own * rows, width), client_ids, labels, ext_weight, bias, wn, bn,
         embeddings, hin_t, hyper_bias[None], ho, n_dp, n_hyper, aligned,
     )
     grad_out, gw, gb, table, grad_in, grad_hb = last_part(
-        dheads, hid, pre, picked, select, hin_t, dh.reshape(-1, 128), gw_all, aligned
+        go, pre, picked, select, hin_t, dh.reshape(-1, 128), gw_all, aligned
     )
     if not aligned:
         gw = gw_all[:, :, :width].transpose(2, 1, 0, 3).reshape(width, -1).astype(f32)

time: 88.6 us -> 78.8 us (0.89)
  Pallas kernels: 84.9 us -> 77.8 us
  local copies, waits for them, and re-layouts: 2.4 us -> 0 us
    pallas_call x1, Pallas kernels: 11.4 us -> 6.04 us  [last_part(): pl.pallas_call(functools.partial(last_kernel, aligned), grid=(wide // per...]
    broadcast_in_dim x3 -> x0, local copies, waits for them, and re-layouts: 2.4 us -> none  [the longest x1 1.31 us: local(): bias = ext_bias[None]]
    pallas_call x1, Pallas kernels: 73.6 us -> 71.8 us  [main_part(): pl.pallas_call(functools.partial(main_kernel, n_dp, half, own, rows, alig...]
where the time goes in v3:
time: 78.8 us; the launch traced here: 78.4 us
  Pallas kernels  77.8 us (99%)
    pallas_call x1, Pallas kernels, main_part(): pl.pallas_call(functools.partial(main_kernel, n_dp, half, own, rows, alig...  71.8 us
    pallas_call x1, Pallas kernels, last_part(): pl.pallas_call(functools.partial(last_kernel, aligned), grid=(wide // per...  6.04 us

profile of v3, /device:TPU:0, one launch (start us, length us, event | category | flops | bytes accessed | tf_op | source)
XLA Modules:
  0.0 78.4 jit_solution(10614010795641039115)
XLA Ops:
  0.6 71.8 %main_part.1 = (bf16[8,4,144,128]{3,2,1,0:T(8,128)(2,1)}, f32[4,16,128]{2,1,0:T(8,128)}, bf16[50,128,256]{2,1,0:T(8,128)(2,1)}, f32[64,50]{1,0:T(8,128)}, bf16[6...) custom-call(bf16[128,128]{1,0:T(8,128)(2,1)} %bitcast.12, s32[2]{0:T(128)} %ids_ref.1, s32[2,64]{1,0:T(2,128)} %lab_ref.1, ...), custom_call_target="tpu_custom_call" | custom-call | tf_op jit(solution)/shard_map/main_part/pallas_call | solution.py:581
  72.4 6.0 %last_part.1 = (f32[50,128,256]{2,1,0:T(8,128)}, f32[128,4096]{1,0:T(8,128)}, f32[1,4096]{1,0:T(1,128)}, f32[64,128]{1,0:T(8,128)}, f32[50,128]{1,0:T(8,128)}, /*index=5*/f32[1,50]{1,0:T(1,128)}) custom-call(bf16[50,128,256]{2,1,0:T(8,128)(2,1)} %get-tuple-element.18.go_ref, f32[64,50]{1,0:T(8,128)} %get-tuple-element.19.pre_ref, ...), custom_call_target="tpu_custom_call" | custom-call | tf_op jit(solution)/shard_map/last_part/pallas_call | solution.py:686

commit v4 on v3

--- a/solution.py
+++ b/solution.py
@@ -13,6 +13,7 @@
 i32 = jnp.int32
 VM = pl.BlockSpec(memory_space=pltpu.VMEM)
 DG = 16
+HG = 8
 LIMIT = 60 * 1024 * 1024
 
 
@@ -50,15 +51,28 @@
 
 def spread(hidden):
     k, h = hidden.shape
-    rows = lax.broadcasted_iota(i32, (k * DG, k), 0) // DG
-    pick = (rows == lax.broadcasted_iota(i32, (k * DG, k), 1)).astype(bf16)
+    rows = lax.broadcasted_iota(i32, (k * HG, k), 0) // HG
+    pick = (rows == lax.broadcasted_iota(i32, (k * HG, k), 1)).astype(bf16)
     tall = dot(pick, hidden).astype(bf16)
-    columns = lax.broadcasted_iota(i32, (h, h * DG), 1) // DG
-    widen = (columns == lax.broadcasted_iota(i32, (h, h * DG), 0)).astype(bf16)
+    columns = lax.broadcasted_iota(i32, (h, h * HG), 1) // HG
+    widen = (columns == lax.broadcasted_iota(i32, (h, h * HG), 0)).astype(bf16)
     full = dot(tall, widen)
-    d = lax.broadcasted_iota(i32, full.shape, 0) % DG
-    same = d == lax.broadcasted_iota(i32, full.shape, 1) % DG
+    d = lax.broadcasted_iota(i32, full.shape, 0) % HG
+    same = d == lax.broadcasted_iota(i32, full.shape, 1) % HG
     return jnp.where(same, full, 0.0).astype(bf16)
+
+
+def halves(tiles):
+    h, _, c = tiles.shape
+    split = tiles.astype(f32).reshape(h, 2, HG, c)
+    return [split[:, n].reshape(h * HG, c).astype(bf16) for n in range(2)]
+
+
+def build_heads(diag, tiles):
+    parts = [dot(diag, half) for half in halves(tiles)]
+    k = diag.shape[0] // HG
+    parts = [part.reshape(k, 1, HG, part.shape[1]) for part in parts]
+    return jnp.concatenate(parts, axis=1).reshape(k, 2 * HG, parts[0].shape[3]).astype(bf16)
 
 
 def spread_t(hidden):
@@ -208,7 +222,7 @@
     depth = bufs.shape[0]
     slots = n_dp * n_hyper * own
     group = n_hyper * own
-    CS = diag.shape[0] // DG
+    CS = diag.shape[0] // HG
 
     def buffer(c, slot):
         at = pl.ds(pl.multiple_of(c * chunk, chunk), chunk)
@@ -271,9 +285,8 @@
         slot = lax.rem(c, depth)
         buffer(c, slot).wait()
         for g in range(chunk // DG):
-            rhs = bufs[slot, :, g * DG : (g + 1) * DG, :].reshape(hh * DG, classes)
-            out = dot(diag_f[...], rhs).astype(bf16)
-            heads_f[:, g * DG : (g + 1) * DG, :] = out.reshape(group, DG, classes)
+            spot = slice(g * DG, (g + 1) * DG)
+            heads_f[:, spot, :] = build_heads(diag_f[...], bufs[slot, :, spot, :])
 
         @pl.when(c + depth < chunks)
         def _():
@@ -380,8 +393,8 @@
 
     def heads_part(low, high):
         def step(g, carry):
-            out = dot(diag[...], ho_group(g)).astype(bf16)
-            heads[:, pl.ds(pl.multiple_of(g * DG, DG), DG), :] = out.reshape(CS, DG, classes)
+            at = pl.ds(pl.multiple_of(g * DG, DG), DG)
+            heads[:, at, :] = build_heads(diag[...], ho_n[:, at, :])
             return carry
 
         lax.fori_loop(low, high, step, 0)
@@ -599,13 +612,13 @@
             vm((width, narrow), bf16),
             vm((depth, hh, chunk, classes), bf16),
             vm((hh, narrow, classes), bf16),
-            vm((group * DG, hh * DG), bf16),
+            vm((group * HG, hh * HG), bf16),
             vm((group, chunk, classes), bf16),
             vm((n_hyper, tall, classes), f32),
             vm((half, tall, classes), f32),
             vm((half, tall, classes), f32),
             vm((half, tall, classes), f32),
-            vm((CS * DG, hh * DG), bf16),
+            vm((CS * HG, hh * HG), bf16),
             vm((CS, narrow, classes), bf16),
             vm((narrow // DG, slots * DG, classes), bf16),
             vm((hh * DG, CS * DG), bf16),
@@ -639,73 +652,77 @@
     )(x, ids, labels, ew, eb, wn, bn, emb, hin_t, hb, ho)
 
 
-def last_kernel(aligned, go_ref, pre_ref, picked_ref, select_ref, hin_ref, dh_ref, gw_ref,
-                go_out, gwf_out, gb_ref, table_ref, in_ref, hb_ref, gwf_ref, sem):
-    hh = go_ref.shape[0]
-    last = pl.num_programs(0) - 1
-
-    @pl.when(pl.program_id(0) == jnp.minimum(1, last))
-    def _():
-        if aligned:
-            n_dp, n_hyper, tall, narrow = gw_ref.shape
-            for jj in range(n_hyper):
-                for ii in range(n_dp):
-                    at = (jj * n_dp + ii) * narrow
-                    gwf_ref[:, at : at + narrow] = gw_ref[ii, jj, : tall - 16, :].astype(f32)
-                    gb_ref[:, at : at + narrow] = gw_ref[ii, jj, tall - 16 : tall - 8, :].astype(f32)[:1]
-            pltpu.make_async_copy(gwf_ref, gwf_out, sem).start()
-
-    @pl.when(pl.program_id(0) == jnp.minimum(2, last))
-    def _():
-        dpre = dh_ref[...][:, :hh] * silu_slope(pre_ref[...])
-        hb_ref[...] = jnp.sum(dpre, axis=0, keepdims=True)
-        in_ref[...] = dot(dpre, picked_ref[...].astype(f32), ((0,), (0,)), precision=highest)
-        back = dot(dpre, hin_ref[...].astype(f32), precision=highest)
-        table_ref[...] = dot(select_ref[...].astype(f32), back, ((0,), (0,)), precision=highest)
-
-    go_out[...] = go_ref[...].astype(f32)
-
-    @pl.when(pl.program_id(0) == last)
-    def _():
-        if aligned:
-            pltpu.make_async_copy(gwf_ref, gwf_out, sem).wait()
+def last_kernel(aligned, pieces, go_in, gw_in, pre_ref, picked_ref, select_ref, hin_ref, dh_ref,
+                go_out, gwf_out, gb_ref, table_ref, in_ref, hb_ref, go_b, go_f, gw_ref, gwf_ref, sems):
+    hh, wide, _ = go_b.shape
+    per = wide // pieces
+    reads, writes = [], []
+    for n in range(pieces):
+        at = slice(n * per, (n + 1) * per)
+        reads.append(pltpu.make_async_copy(go_in.at[:, at, :], go_b.at[:, at, :], sems.at[0, n]))
+        writes.append(pltpu.make_async_copy(go_f.at[:, at, :], go_out.at[:, at, :], sems.at[1, n]))
+        reads[n].start()
+    get = pltpu.make_async_copy(gw_in, gw_ref, sems.at[2, 0])
+    put = pltpu.make_async_copy(gwf_ref, gwf_out, sems.at[2, 1])
+    if aligned:
+        get.start()
+    for n in range(pieces):
+        at = slice(n * per, (n + 1) * per)
+        reads[n].wait()
+        go_f[:, at, :] = go_b[:, at, :].astype(f32)
+        writes[n].start()
+    if aligned:
+        get.wait()
+        n_dp, n_hyper, tall, narrow = gw_ref.shape
+        for jj in range(n_hyper):
+            for ii in range(n_dp):
+                at = (jj * n_dp + ii) * narrow
+                gwf_ref[:, at : at + narrow] = gw_ref[ii, jj, : tall - 16, :].astype(f32)
+                gb_ref[:, at : at + narrow] = gw_ref[ii, jj, tall - 16 : tall - 8, :].astype(f32)[:1]
+        put.start()
+    dpre = dh_ref[...][:, :hh] * silu_slope(pre_ref[...])
+    hb_ref[...] = jnp.sum(dpre, axis=0, keepdims=True)
+    in_ref[...] = dot(dpre, picked_ref[...].astype(f32), ((0,), (0,)), precision=highest)
+    back = dot(dpre, hin_ref[...].astype(f32), precision=highest)
+    table_ref[...] = dot(select_ref[...].astype(f32), back, ((0,), (0,)), precision=highest)
+    for copy in writes:
+        copy.wait()
+    if aligned:
+        put.wait()
 
 
 def last_part(go, pre, picked, select, hin_t, dh, gw_all, aligned):
     hh, wide, classes = go.shape
-    slots, width = picked.shape
+    width = picked.shape[1]
     clients = select.shape[1]
     n_dp, n_hyper, block, narrow = gw_all.shape
-    whole = lambda *s: pl.BlockSpec(s, lambda g: (0,) * len(s))
     shape = jax.ShapeDtypeStruct
     full = (block - 16, n_dp * n_hyper * narrow) if aligned else (8, 128)
-    bias = (1, full[1])
     given = gw_all if aligned else gw_all[:1, :1]
-    per = 32 if wide % 32 == 0 else wide
-    cut = pl.BlockSpec((hh, per, classes), lambda g: (0, g, 0))
+    pieces = 4 if wide % 64 == 0 else 1
+    ANY = pl.BlockSpec(memory_space=pl.ANY)
     return pl.pallas_call(
-        functools.partial(last_kernel, aligned),
-        grid=(wide // per,),
+        functools.partial(last_kernel, aligned, pieces),
         out_shape=(
             shape(go.shape, f32),
             shape(full, f32),
-            shape(bias, f32),
+            shape((1, full[1]), f32),
             shape((clients, hin_t.shape[1]), f32),
             shape((hh, width), f32),
             shape((1, hh), f32),
         ),
-        in_specs=[
-            cut, whole(slots, hh), whole(slots, width), whole(slots, clients),
-            whole(*hin_t.shape), whole(slots, 128), whole(*given.shape),
+        in_specs=[ANY, ANY, VM, VM, VM, VM, VM],
+        out_specs=(ANY, ANY, VM, VM, VM, VM),
+        scratch_shapes=[
+            pltpu.VMEM(go.shape, bf16),
+            pltpu.VMEM(go.shape, f32),
+            pltpu.VMEM(given.shape, bf16),
+            pltpu.VMEM(full, f32),
+            pltpu.SemaphoreType.DMA((3, 4)),
         ],
-        out_specs=[
-            cut, pl.BlockSpec(memory_space=pl.ANY),
-            whole(*bias), whole(clients, hin_t.shape[1]), whole(hh, width), whole(1, hh),
-        ],
-        scratch_shapes=[pltpu.VMEM(full, f32), pltpu.SemaphoreType.DMA],
         compiler_params=pltpu.CompilerParams(vmem_limit_bytes=LIMIT),
         name="last_part",
-    )(go, pre, picked, select, hin_t, dh, given)
+    )(go, given, pre, picked, select, hin_t, dh)
 
 
 def local(

time: 78.8 us -> 78.1 us (level)
    pallas_call x1, Pallas kernels: 71.8 us -> 70.8 us  [main_part(): pl.pallas_call(functools.partial(main_kernel, n_dp, half, own, rows, alig...]
where the time goes in v4:
time: 78.1 us; the launch traced here: 77.7 us
  Pallas kernels  77.1 us (99%)
    pallas_call x1, Pallas kernels, main_part(): pl.pallas_call(functools.partial(main_kernel, n_dp, half, own, rows, alig...  70.8 us
    pallas_call x1, Pallas kernels, last_part(): pl.pallas_call(functools.partial(last_kernel, aligned, pieces), out_shape...  6.24 us

profile of v4, /device:TPU:0, one launch (start us, length us, event | category | flops | bytes accessed | tf_op | source)
XLA Modules:
  0.0 77.7 jit_solution(5300149138789317229)
XLA Ops:
  0.6 70.8 %main_part.1 = (bf16[8,4,144,128]{3,2,1,0:T(8,128)(2,1)}, f32[4,16,128]{2,1,0:T(8,128)}, bf16[50,128,256]{2,1,0:T(8,128)(2,1)}, f32[64,50]{1,0:T(8,128)}, bf16[6...) custom-call(bf16[128,128]{1,0:T(8,128)(2,1)} %bitcast.12, s32[2]{0:T(128)} %ids_ref.1, s32[2,64]{1,0:T(2,128)} %lab_ref.1, ...), custom_call_target="tpu_custom_call" | custom-call | tf_op jit(solution)/shard_map/main_part/pallas_call | solution.py:594
  71.5 6.2 %last_part.1 = (f32[50,128,256]{2,1,0:T(8,128)}, f32[128,4096]{1,0:T(8,128)}, f32[1,4096]{1,0:T(1,128)}, f32[64,128]{1,0:T(8,128)}, f32[50,128]{1,0:T(8,128)}, /*index=5*/f32[1,50]{1,0:T(1,128)}) custom-call(bf16[50,128,256]{2,1,0:T(8,128)(2,1)} %get-tuple-element.18.go_in, bf16[8,4,144,128]{3,2,1,0:T(8,128)(2,1)} %get-tuple-element.19.gw_in, ...), custom_call_target="tpu_custom_call" | custom-call | tf_op jit(solution)/shard_map/last_part/pallas_call | solution.py:704

commit v5 on v4

--- a/solution.py
+++ b/solution.py
@@ -49,10 +49,13 @@
     return i, j, j + 1 - 2 * lax.rem(j, 2)
 
 
-def spread(hidden):
+def spread(hidden, slots=0, own=0):
     k, h = hidden.shape
-    rows = lax.broadcasted_iota(i32, (k * HG, k), 0) // HG
-    pick = (rows == lax.broadcasted_iota(i32, (k * HG, k), 1)).astype(bf16)
+    slots = slots or k
+    rows = lax.broadcasted_iota(i32, (slots * HG, k), 0) // HG
+    if own:
+        rows = rows // own * 16 + rows % own
+    pick = (rows == lax.broadcasted_iota(i32, (slots * HG, k), 1)).astype(bf16)
     tall = dot(pick, hidden).astype(bf16)
     columns = lax.broadcasted_iota(i32, (h, h * HG), 1) // HG
     widen = (columns == lax.broadcasted_iota(i32, (h, h * HG), 0)).astype(bf16)
@@ -249,18 +252,19 @@
         number = ids_ref[s]
         tile = jnp.where(row == s, (number // 256).astype(f32), tile)
         tile = jnp.where(row == 8 + s, (number % 256).astype(f32), tile)
-    packed[:tall] = x_ref[...]
-    packed[tall:] = tile.astype(bf16)
-    id_own[...] = tile.astype(bf16)
-    id_all[j] = tile.astype(bf16)
-    xg[i, j, :tall] = x_ref[...]
-    xg[i, j, tall:] = tile.astype(bf16)
-
     sem = pltpu.get_barrier_semaphore()
     others = [(swap(i, t, n_dp), j) for t in range(1, n_dp)]
     others += [(i, lax.rem(j + u, n_hyper)) for u in range(1, n_hyper)]
     for dp, hyper in others:
         pl.semaphore_signal(sem, 1, device_id={"dp": dp, "hyper": hyper})
+    packed[:tall] = x_ref[...]
+    packed[tall:] = tile.astype(bf16)
+    small = (emb_ref[...], hin_ref[...], hb_ref[...])
+    id_own[...] = jnp.zeros_like(id_own)
+    id_own[:own, :hh] = hypernet(tile.astype(bf16)[None], own, *small)[3]
+    id_all[j] = id_own[...]
+    xg[i, j, :tall] = x_ref[...]
+    xg[i, j, tall:] = tile.astype(bf16)
     pl.semaphore_wait(sem, len(others))
 
     na = n_dp // 2
@@ -273,8 +277,7 @@
     inp.begin(packed)
     for copy in to_ids:
         copy.wait_recv()
-    small = (emb_ref[...], hin_ref[...], hb_ref[...])
-    diag_f[...] = spread(hypernet(id_all[...], own, *small)[3])
+    diag_f[...] = spread(id_all[...].reshape(n_hyper * 16, width)[:, :hh], group, own)
     part[...] = jnp.zeros_like(part)
     bias_w[...] = eb_ref[pl.ds(pl.multiple_of(j * wide, 256), wide)].astype(f32)[None]
     get_w.wait()

time: 78.1 us -> 77.8 us (level)
  no operation moved by 1% of the time
where the time goes in v5:
time: 77.8 us; the launch traced here: 77.5 us
  Pallas kernels  76.9 us (99%)
    pallas_call x1, Pallas kernels, main_part(): pl.pallas_call(functools.partial(main_kernel, n_dp, half, own, rows, alig...  70.6 us
    pallas_call x1, Pallas kernels, last_part(): pl.pallas_call(functools.partial(last_kernel, aligned, pieces), out_shape...  6.24 us

profile of v5, /device:TPU:0, one launch (start us, length us, event | category | flops | bytes accessed | tf_op | source)
XLA Modules:
  0.0 77.5 jit_solution(10304848128281503522)
XLA Ops:
  0.6 70.6 %main_part.1 = (bf16[8,4,144,128]{3,2,1,0:T(8,128)(2,1)}, f32[4,16,128]{2,1,0:T(8,128)}, bf16[50,128,256]{2,1,0:T(8,128)(2,1)}, f32[64,50]{1,0:T(8,128)}, bf16[6...) custom-call(bf16[128,128]{1,0:T(8,128)(2,1)} %bitcast.12, s32[2]{0:T(128)} %ids_ref.1, s32[2,64]{1,0:T(2,128)} %lab_ref.1, ...), custom_call_target="tpu_custom_call" | custom-call | tf_op jit(solution)/shard_map/main_part/pallas_call | solution.py:597
  71.3 6.2 %last_part.1 = (f32[50,128,256]{2,1,0:T(8,128)}, f32[128,4096]{1,0:T(8,128)}, f32[1,4096]{1,0:T(1,128)}, f32[64,128]{1,0:T(8,128)}, f32[50,128]{1,0:T(8,128)}, /*index=5*/f32[1,50]{1,0:T(1,128)}) custom-call(bf16[50,128,256]{2,1,0:T(8,128)(2,1)} %get-tuple-element.18.go_in, bf16[8,4,144,128]{3,2,1,0:T(8,128)(2,1)} %get-tuple-element.19.gw_in, ...), custom_call_target="tpu_custom_call" | custom-call | tf_op jit(solution)/shard_map/last_part/pallas_call | solution.py:707
